TPU v7x, 128 devices: a whole 4x4x4 slice. The times are simulated.
128 devices in a mesh: depth: 4 (over y), row: 4 (over x), col: 8 (over z, core).
Axes of the slice: x: 4, y: 4, z: 4, core: 2. Of those that a mesh axis runs over, the one named last changes fastest.
Arguments:
- alignment: bfloat16 [256, 512, 256], P('depth', ('row', 'col')), may hold values from -6 to 6
- norm_gain: float32 [256], replicated, may hold values from 0.25 to 1.75
- norm_shift: float32 [256], replicated, may hold values from -3 to 3
- proj_weight: bfloat16 [256, 64], replicated, may hold values from -0.375 to 0.375
- proj_bias: float32 [64], replicated, may hold values from -3 to 3
- out_weight: bfloat16 [1024, 128], replicated, may hold values from -0.1875 to 0.1875
- out_bias: float32 [128], replicated, may hold values from -3 to 3
- cotangent: bfloat16 [512, 512, 128], P('row', 'col', 'depth'), may hold values from -6 to 6
Outputs:
- pair_update: bfloat16 [512, 512, 128], P('row', 'col', 'depth')
- grad_alignment: bfloat16 [256, 512, 256], P('depth', ('row', 'col'))
- grad_proj_weight: float32 [256, 64], replicated
- grad_proj_bias: float32 [64], replicated
- grad_out_weight: float32 [1024, 128], replicated
- grad_out_bias: float32 [128], replicated
- grad_norm_gain: float32 [256], replicated
- grad_norm_shift: float32 [256], replicated
All inputs are finite; a program needn't handle non-finite values.
Results may differ from a plain program's by a relative error of at most 0.009.
Values may be sent and summed in bfloat16 or wider, within the bound.
No kernel may reach another device: no remote copies, remote signals or barrier semaphores. Data moves between devices by JAX's collectives and lax.ppermute only.
A program may use at most 64 MiB of HBM per device.

v0:
```python
import jax
import jax.numpy as jnp
from jax import lax
from jax.experimental import pallas as pl
from jax.experimental.pallas import tpu as pltpu
from jax.sharding import Mesh
from jax.sharding import PartitionSpec as P

EPSILON = 1e-05
F32 = jnp.float32
BF16 = jnp.bfloat16
NN = (((1,), (0,)), ((), ()))
NT = (((1,), (1,)), ((), ()))
TN = (((0,), (0,)), ((), ()))


def dot(a, b, dims):
    return lax.dot_general(a, b, dims, preferred_element_type=F32)


def vmem(count):
    return [pl.BlockSpec(memory_space=pltpu.VMEM)] * count


def hbm(count):
    return [pl.BlockSpec(memory_space=pltpu.HBM)] * count


def cost(us):
    return pl.CostEstimate(flops=us * 400_000_000, bytes_accessed=1_000_000, transcendentals=0)


def limit(mib):
    return pltpu.CompilerParams(vmem_limit_bytes=mib * 2**20)


def column_of(row):
    size = row.shape[1]
    on = lax.broadcasted_iota(jnp.int32, (size, size), 0) == lax.broadcasted_iota(
        jnp.int32, (size, size), 1
    )
    return jnp.sum(jnp.where(on, row, 0.0), axis=1, keepdims=True)


def sides_kernel(
    x_ref, gain_ref, shift_ref, wt_ref, bias_ref, left_ref, right_ref, normed_ref, rows, packed
):
    seqs, own = 64, 16
    gain, shift = gain_ref[...], shift_ref[...]

    def block(k, _):
        x = x_ref[pl.ds(k * 128, 128), :].astype(F32)
        centre = x - jnp.mean(x, axis=-1, keepdims=True)
        spread = jnp.mean(centre * centre, axis=-1, keepdims=True)
        hat = centre * lax.rsqrt(spread + EPSILON)
        rows[0, pl.ds(k * 128, 128), :] = hat[:, :128]
        rows[1, pl.ds(k * 128, 128), :] = hat[:, 128:]
        return 0

    lax.fori_loop(0, 8, block, 0)
    for i in range(own):
        hat = jnp.concatenate(
            [rows[h, pl.ds(i, seqs, stride=own), :] for h in range(2)], axis=1
        )
        at = slice(i * seqs, (i + 1) * seqs)
        normed_ref[at, :256] = (hat * gain + shift).astype(BF16)
        normed_ref[at, 256:] = hat.astype(BF16)
    sides = dot(wt_ref[...], normed_ref[:, :256], NT) + column_of(bias_ref[...])
    for i in range(own):
        t = sides[:, i * seqs : (i + 1) * seqs]
        for side in range(2):
            lo = t[side * 32 : side * 32 + 16]
            hi = t[side * 32 + 16 : side * 32 + 32]
            packed[pl.ds(side * 256 + i, 16, stride=own), :] = jnp.concatenate([lo, hi], axis=1)
    left = packed[:256, :].astype(BF16).reshape(16, own, 128)
    for peer in range(16):
        left_ref[peer] = left
    right_ref[...] = packed[256:, :].astype(BF16).reshape(16, own, 128)


def sides_call(x, gain, shift, wt, bias):
    return pl.pallas_call(
        sides_kernel,
        out_shape=(
            jax.ShapeDtypeStruct((16, 16, 16, 128), BF16),
            jax.ShapeDtypeStruct((16, 16, 128), BF16),
            jax.ShapeDtypeStruct((1024, 512), BF16),
        ),
        in_specs=vmem(5),
        out_specs=tuple(vmem(3)),
        scratch_shapes=[pltpu.VMEM((2, 1024, 128), F32), pltpu.VMEM((512, 128), F32)],
        cost_estimate=cost(4),
        name="sides",
    )(x, gain, shift, wt, bias)


def grad_kernel(s_ref, w_ref, gp_ref, st_ref, gb_ref, tall, held, sems):
    ones = lax.broadcasted_iota(jnp.int32, (128, 128), 0) == lax.broadcasted_iota(
        jnp.int32, (128, 128), 1
    )
    columns = []
    for d in range(4):
        count = jnp.zeros((32, 128), F32)
        for j in range(16):
            t = s_ref[d, j].astype(F32)
            count = count + t
            st_ref[d * 32 : (d + 1) * 32, j * 128 : (j + 1) * 128] = (t * (1.0 / 256)).astype(
                BF16
            )
        columns.append(jnp.sum(count, axis=1, keepdims=True))
    column = jnp.concatenate(columns, axis=0)
    gb_ref[...] = jnp.sum(jnp.where(ones, column, 0.0), axis=0, keepdims=True)

    for j in range(0, 16, 2):
        g = dot(w_ref[...], st_ref[:, j * 128 : (j + 2) * 128], NN)
        for jj in range(2):
            tall[:, (j + jj) * 8 : (j + jj + 1) * 8, :] = g[
                :, jj * 128 : (jj + 1) * 128
            ].reshape(128, 8, 128)

    def relay(c, _):
        for e in range(32):
            held[c, e * 16 : (e + 1) * 16, :] = tall[
                c * 4 + e // 8, pl.ds(e % 8, 16, stride=8), :
            ].astype(BF16)
        return 0

    copies = []
    for q in range(4):
        lax.fori_loop(q * 8, (q + 1) * 8, relay, 0)
        part = pl.ds(q * 8, 8)
        copies.append(pltpu.make_async_copy(held.at[part], gp_ref.at[part], sems.at[q]))
        copies[-1].start()
    for copy in copies:
        copy.wait()


def grad_call(s, w):
    return pl.pallas_call(
        grad_kernel,
        out_shape=(
            jax.ShapeDtypeStruct((32, 512, 128), BF16),
            jax.ShapeDtypeStruct((128, 2048), BF16),
            jax.ShapeDtypeStruct((1, 128), F32),
        ),
        in_specs=vmem(2),
        out_specs=(*hbm(1), *vmem(2)),
        scratch_shapes=[
            pltpu.VMEM((128, 128, 128), F32),
            pltpu.VMEM((32, 512, 128), BF16),
            pltpu.SemaphoreType.DMA((4,)),
        ],
        cost_estimate=cost(5),
        name="grad",
    )(s, w)


def left_kernel(
    r0_ref, r1_ref, r2_ref, r3_ref, gp_ref, keep_ref, send_ref, rt_ref,
    rbuf, held, sems, keep, send, out_sems,
):
    copies = []
    for q in range(8):
        part = pl.ds((q // 2 + q % 2 * 4) * 4, 4)
        copies.append(pltpu.make_async_copy(gp_ref.at[part], held.at[part], sems.at[q]))
        copies[-1].start()
    core = lax.axis_index("col_1")
    row = lax.axis_index("row")
    for m, ref in enumerate((r0_ref, r1_ref, r2_ref, r3_ref)):
        rbuf[lax.rem(row - m + 4, 4)] = ref[...].reshape(256, 128)
    for eh in range(2):
        for half in range(2):
            cut = [rbuf[2 * half + y][:, eh * 64 : eh * 64 + 64] for y in range(2)]
            rt_ref[eh * 256 : (eh + 1) * 256, half * 128 : (half + 1) * 128] = jnp.concatenate(
                cut, axis=1
            )

    def left(k, _):
        sums = [dot(held[ch * 16 + k], rt_ref[...], TN) for ch in range(2)]
        for y in range(4):
            t = jnp.concatenate([v[:, y * 64 : (y + 1) * 64] for v in sums], axis=1)
            for z in range(4):
                a = t[z * 32 : z * 32 + 16]
                b = t[z * 32 + 16 : z * 32 + 32]
                keep[y * 4 + z, k] = jnp.where(core == 0, a, b).astype(BF16)
                send[y * 4 + z, k] = jnp.where(core == 0, b, a).astype(BF16)
        return 0

    outs = []
    for q in range(4):
        copies[2 * q].wait()
        copies[2 * q + 1].wait()
        lax.fori_loop(q * 4, (q + 1) * 4, left, 0)
        part = pl.ds(q * 4, 4)
        outs.append(pltpu.make_async_copy(send.at[:, part], send_ref.at[:, part], out_sems.at[2 * q]))
        outs.append(pltpu.make_async_copy(keep.at[:, part], keep_ref.at[:, part], out_sems.at[2 * q + 1]))
        outs[-2].start()
        outs[-1].start()
    for copy in outs:
        copy.wait()


def left_call(rs, gp):
    return pl.pallas_call(
        left_kernel,
        out_shape=(
            jax.ShapeDtypeStruct((16, 16, 16, 128), BF16),
            jax.ShapeDtypeStruct((16, 16, 16, 128), BF16),
            jax.ShapeDtypeStruct((512, 256), BF16),
        ),
        in_specs=(*vmem(4), *hbm(1)),
        out_specs=(*hbm(2), *vmem(1)),
        scratch_shapes=[
            pltpu.VMEM((4, 256, 128), BF16),
            pltpu.VMEM((32, 512, 128), BF16),
            pltpu.SemaphoreType.DMA((8,)),
            pltpu.VMEM((16, 16, 16, 128), BF16),
            pltpu.VMEM((16, 16, 16, 128), BF16),
            pltpu.SemaphoreType.DMA((8,)),
        ],
        cost_estimate=cost(5),
        name="left",
    )(*rs, gp)


def right_kernel(
    near_ref, far_ref, gp_ref, g0_ref, g1_ref, g2_ref, g3_ref, lt_ref,
    gbuf, held, sems, near, far, lt,
):
    sides = [
        pltpu.make_async_copy(near_ref, near, sems.at[4]),
        pltpu.make_async_copy(far_ref, far, sems.at[5]),
    ]
    for copy in sides:
        copy.start()
    copies = []
    for q in range(4):
        part = pl.ds(q * 8, 8)
        copies.append(pltpu.make_async_copy(gp_ref.at[part], held.at[part], sems.at[q]))
        copies[-1].start()
    for copy in sides:
        copy.wait()
    core = lax.axis_index("col_1")
    row = lax.axis_index("row")

    def merge(k, _):
        for ref, side in ((near, core), (far, 1 - core)):
            for z in range(4):
                parts = [ref[y * 4 + z, k] for y in range(4)]
                for ch in range(2):
                    cut = [p[:, ch * 64 : ch * 64 + 64] for p in parts]
                    at = pl.multiple_of((ch * 16 + k) * 128 + (2 * z + side) * 16, 16)
                    lt[pl.ds(at, 16), 0:128] = jnp.concatenate(cut[:2], axis=1)
                    lt[pl.ds(at, 16), 128:256] = jnp.concatenate(cut[2:], axis=1)
        return 0

    lax.fori_loop(0, 16, merge, 0)
    kept = pltpu.make_async_copy(lt, lt_ref, sems.at[6])
    kept.start()

    for copy in copies:
        copy.wait()
    wide = jnp.concatenate([held[c] for c in range(32)], axis=1)
    total = dot(wide, lt[...], NN)
    for y in range(4):
        t = jnp.concatenate(
            [total[eh * 256 : (eh + 1) * 256, y * 64 : (y + 1) * 64] for eh in range(2)], axis=1
        )
        gbuf[y] = t.astype(BF16)
    for m, ref in enumerate((g0_ref, g1_ref, g2_ref, g3_ref)):
        ref[...] = gbuf[lax.rem(row + m, 4)].reshape(16, 16, 128)
    kept.wait()


def right_call(near, far, gp):
    return pl.pallas_call(
        right_kernel,
        out_shape=(
            *[jax.ShapeDtypeStruct((16, 16, 128), BF16)] * 4,
            jax.ShapeDtypeStruct((4096, 256), BF16),
        ),
        in_specs=hbm(3),
        out_specs=(*vmem(4), *hbm(1)),
        scratch_shapes=[
            pltpu.VMEM((4, 256, 128), BF16),
            pltpu.VMEM((32, 512, 128), BF16),
            pltpu.SemaphoreType.DMA((7,)),
            pltpu.VMEM((16, 16, 16, 128), BF16),
            pltpu.VMEM((16, 16, 16, 128), BF16),
            pltpu.VMEM((4096, 256), BF16),
        ],
        cost_estimate=cost(5),
        name="right",
    )(near, far, gp)


def outer_kernel(
    lt_ref, rt_ref, st_ref, w_ref, bias_ref, pair_ref, gw_ref, tall, xs, lt, sems
):
    copies = []
    for q in range(4):
        part = pl.ds(q * 1024, 1024)
        copies.append(pltpu.make_async_copy(lt_ref.at[part], lt.at[part], sems.at[q]))
        copies[-1].start()
    bias = column_of(bias_ref[...])

    def outer(k, _):
        both = lt[pl.ds(pl.multiple_of(k * 256, 256), 256), :]
        o = dot(rt_ref[...], both, NT)
        for ch in range(2):
            for e in range(32):
                tall[k * 8 + ch * 4 + e // 8, pl.ds(e % 8, 16, stride=8), :] = o[
                    e * 16 : (e + 1) * 16, ch * 128 : (ch + 1) * 128
                ]
        return 0

    for q in range(4):
        copies[q].wait()
        lax.fori_loop(q * 4, (q + 1) * 4, outer, 0)

    def convert(k, _):
        for j in range(16):
            xs[pl.ds(pl.multiple_of(k * 64, 64), 64), j * 128 : (j + 1) * 128] = (
                tall[pl.ds(k * 8, 8), j * 8 : (j + 1) * 8, :].reshape(64, 128).astype(BF16)
            )
        return 0

    lax.fori_loop(0, 16, convert, 0)

    for j in range(0, 16, 2):
        part = dot(w_ref[...], xs[:, j * 128 : (j + 2) * 128], TN)
        part = (part * (1.0 / 256) + bias).astype(BF16)
        for jj in range(2):
            for d in range(4):
                pair_ref[d, j + jj] = part[d * 32 : (d + 1) * 32, jj * 128 : (jj + 1) * 128]

    def weight(k, _):
        at = pl.multiple_of(k * 256, 256)
        gw_ref[pl.ds(at, 256), :] = dot(xs[pl.ds(at, 256), :], st_ref[...], NT).astype(BF16)
        return 0

    lax.fori_loop(0, 4, weight, 0)


def outer_call(lt, rt, st, w, bias):
    return pl.pallas_call(
        outer_kernel,
        out_shape=(
            jax.ShapeDtypeStruct((4, 16, 32, 128), BF16),
            jax.ShapeDtypeStruct((1024, 128), BF16),
        ),
        in_specs=(*hbm(1), *vmem(4)),
        out_specs=tuple(vmem(2)),
        scratch_shapes=[
            pltpu.VMEM((128, 128, 128), F32),
            pltpu.VMEM((1024, 2048), BF16),
            pltpu.VMEM((4096, 256), BF16),
            pltpu.SemaphoreType.DMA((4,)),
        ],
        cost_estimate=cost(11),
        name="outer",
    )(lt, rt, st, w, bias)


def back_kernel(
    gl_ref, gr_ref, normed_ref, wt_ref, count_ref, gw_ref,
    grad_ref, all_ref,
    sums, flat_ref,
):
    own = 16
    left = gl_ref[0].astype(F32)
    for k in range(1, 16):
        left = left + gl_ref[k].astype(F32)
    right = gr_ref[...].astype(F32)
    sums[0:256, :] = left.reshape(256, 128)
    sums[256:512, :] = right.reshape(256, 128)
    for i in range(own):
        t = [sums[pl.ds(side * 256 + i, 16, stride=own), :] for side in range(2)]
        grad_ref[:, i * 64 : (i + 1) * 64] = jnp.concatenate(
            [t[0][:, :64], t[0][:, 64:], t[1][:, :64], t[1][:, 64:]], axis=0
        ).astype(BF16)
    grad = grad_ref[...]
    both = dot(grad, normed_ref[...], NN)
    wt = wt_ref[...].astype(F32)
    column = jnp.sum(grad.astype(F32), axis=1, keepdims=True)
    gain = jnp.sum(both[:, 256:] * wt, axis=0, keepdims=True)
    shift = jnp.sum(column * wt, axis=0, keepdims=True)
    on = lax.broadcasted_iota(jnp.int32, (64, 128), 0) == lax.broadcasted_iota(
        jnp.int32, (64, 128), 1
    )
    bias = jnp.sum(jnp.where(on, column, 0.0), axis=0, keepdims=True)
    rows = [
        count_ref[...], gain[:, :128], gain[:, 128:], shift[:, :128], shift[:, 128:], bias,
    ]
    flat_ref[...] = jnp.zeros((16, 16, 128), F32)
    for k in range(8):
        flat_ref[k, 0:8, :] = both[k * 8 : (k + 1) * 8, :128]
        flat_ref[8 + k, 0:8, :] = both[k * 8 : (k + 1) * 8, 128:256]
    for k, row in enumerate(rows):
        hi = row.astype(BF16).astype(F32)
        flat_ref[k, 8:9, :] = hi
        flat_ref[k, 9:10, :] = row - hi
    for k in range(16):
        all_ref[k, 0:64, :] = gw_ref[k * 64 : (k + 1) * 64, :]
        all_ref[k, 64:80, :] = flat_ref[k].astype(BF16)


def back_call(gl, gr, normed, wt, count, gw):
    return pl.pallas_call(
        back_kernel,
        out_shape=(
            jax.ShapeDtypeStruct((64, 1024), BF16),
            jax.ShapeDtypeStruct((16, 80, 128), BF16),
        ),
        in_specs=vmem(6),
        out_specs=tuple(vmem(2)),
        scratch_shapes=[pltpu.VMEM((512, 128), F32), pltpu.VMEM((16, 16, 128), F32)],
        compiler_params=limit(8),
        cost_estimate=cost(2),
        name="back",
    )(gl, gr, normed, wt, count, gw)


def norm_kernel(x_ref, gain_ref, wt_ref, grad_ref, gx_ref, rows, rstds):
    seqs, own = 64, 16
    gain = gain_ref[...]

    def block(k, _):
        x = x_ref[pl.ds(k * 128, 128), :].astype(F32)
        mean = jnp.mean(x, axis=-1, keepdims=True)
        centre = x - mean
        spread = jnp.mean(centre * centre, axis=-1, keepdims=True)
        rstd = lax.rsqrt(spread + EPSILON)
        y = centre * rstd
        rows[0, pl.ds(k * 128, 128), :] = y[:, :128]
        rows[1, pl.ds(k * 128, 128), :] = y[:, 128:]
        rstds[pl.ds(k * 128, 128), :] = jnp.broadcast_to(rstd, (128, 128))
        return 0

    lax.fori_loop(0, 8, block, 0)
    for i in range(own):
        gn = dot(grad_ref[:, i * seqs : (i + 1) * seqs], wt_ref[...], TN)
        hat = jnp.concatenate(
            [rows[h, pl.ds(i, seqs, stride=own), :] for h in range(2)], axis=1
        )
        rstd = rstds[pl.ds(i, seqs, stride=own), :][:, :1]
        g = gn * gain
        a = jnp.mean(g, axis=-1, keepdims=True)
        b = jnp.mean(g * hat, axis=-1, keepdims=True)
        gx = rstd * (g - a - hat * b)
        for h in range(2):
            rows[h, pl.ds(i, seqs, stride=own), :] = gx[:, h * 128 : (h + 1) * 128]
    for h in range(2):
        gx_ref[:, h * 128 : (h + 1) * 128] = rows[h].astype(BF16)


def norm_call(x, gain, wt, grad):
    return pl.pallas_call(
        norm_kernel,
        out_shape=jax.ShapeDtypeStruct((1024, 256), BF16),
        in_specs=vmem(4),
        out_specs=pl.BlockSpec(memory_space=pltpu.VMEM),
        scratch_shapes=[pltpu.VMEM((2, 1024, 128), F32), pltpu.VMEM((1024, 128), F32)],
        compiler_params=limit(8),
        cost_estimate=cost(5),
        name="norm",
    )(x, gain, wt, grad)


def exchange(value, axis):
    return lax.all_to_all(value, axis, 0, 0, tiled=True)


def swap(value):
    return lax.ppermute(value, "col_1", [(0, 1), (1, 0)])


def place(d, r, c):
    return (d * 4 + r) * 8 + c


def right_pairs():
    return [
        (place(y, r, c), place(c % 4, y, 2 * r + c // 4))
        for y in range(4)
        for r in range(4)
        for c in range(8)
    ]


def rotate(value, axis, by):
    return lax.ppermute(value, axis, [(k, (k + by) % 4) for k in range(4)])


EVERY = ("depth", "row", "col_0", "col_1")
PLANE = ("depth", "row")


def summed(parts):
    return jnp.sum(parts.astype(F32), axis=0)


def give_kernel(a_ref, b_ref, out_ref):
    total = a_ref[...] + b_ref[...]
    row = total[72:73] + total[73:74]
    hi = row.astype(BF16).astype(F32)
    at = lax.broadcasted_iota(jnp.int32, (8, 128), 0)
    tail = jnp.where(at == 0, hi, jnp.where(at == 1, row - hi, 0.0))
    chunk = jnp.concatenate([total[:72], tail], axis=0).astype(BF16)
    for k in range(16):
        out_ref[k] = chunk


def give_call(a, b):
    return pl.pallas_call(
        give_kernel,
        out_shape=jax.ShapeDtypeStruct((16, 80, 128), BF16),
        in_specs=vmem(2),
        out_specs=vmem(1)[0],
        compiler_params=limit(2),
        cost_estimate=cost(1),
        name="give",
    )(a, b)


def finish_kernel(all_ref, gw_ref, pw_ref, pb_ref, ob_ref, gain_ref, shift_ref):
    for k in range(16):
        gw_ref[k * 64 : (k + 1) * 64, :] = all_ref[k, 0:64, :].astype(F32)
    rows = []
    for k in range(8):
        for half in range(2):
            pw_ref[k * 8 : (k + 1) * 8, half * 128 : (half + 1) * 128] = all_ref[
                half * 8 + k, 64:72, :
            ].astype(F32)
        tail = all_ref[k, 72:80, :].astype(F32)
        rows.append(tail[0:1] + tail[1:2])
    ob_ref[...] = rows[0]
    gain_ref[...] = jnp.concatenate(rows[1:3], axis=1)
    shift_ref[...] = jnp.concatenate(rows[3:5], axis=1)
    pb_ref[...] = rows[5][:, :64]


def finish_call(total):
    return pl.pallas_call(
        finish_kernel,
        out_shape=(
            jax.ShapeDtypeStruct((1024, 128), F32),
            jax.ShapeDtypeStruct((64, 256), F32),
            jax.ShapeDtypeStruct((1, 64), F32),
            jax.ShapeDtypeStruct((1, 128), F32),
            jax.ShapeDtypeStruct((1, 256), F32),
            jax.ShapeDtypeStruct((1, 256), F32),
        ),
        in_specs=vmem(1),
        out_specs=tuple(vmem(6)),
        compiler_params=limit(4),
        cost_estimate=cost(1),
        name="finish",
    )(total)


def step(
    alignment, norm_gain, norm_shift, proj_weight, proj_bias, out_weight, out_bias, cotangent
):
    x = alignment.reshape(1024, 256)
    gain = norm_gain.reshape(1, 256)
    shift = norm_shift.reshape(1, 256)
    wt = proj_weight.T
    cot = exchange(jnp.transpose(cotangent, (1, 2, 0)).reshape(4, 16, 32, 128), "depth")
    left, right, normed = sides_call(x, gain, shift, wt, proj_bias.reshape(1, 64))
    pairs = right_pairs()
    near = exchange(left, ("depth", "col_0"))
    rights = [lax.ppermute(right, EVERY, pairs)]
    for m in range(1, 4):
        rights.append(rotate(rights[0], "row", m))
    far = swap(near)

    gp, st, count = grad_call(cot, out_weight)
    keep, send, rt = left_call(rights, gp)
    came = swap(send)
    mine = (keep.astype(F32) + came.astype(F32)).astype(BF16)
    lefts = exchange(mine, ("depth", "col_0"))

    *gr, lt = right_call(near, far, gp)
    for m in range(1, 4):
        gr[m] = rotate(gr[m], "row", m)
    right_grad = sum(g.astype(F32) for g in gr).astype(BF16)
    right_grad = lax.ppermute(right_grad, EVERY, [(b, a) for a, b in pairs])

    pair, gw = outer_call(lt, rt, st, out_weight, out_bias.reshape(1, 128))
    grad, total = back_call(lefts, right_grad, normed, wt, count, gw)

    total = exchange(total, PLANE)
    total = summed(total)
    for m in (1, 3):
        total = total + lax.ppermute(total, "col_0", [(k, k ^ m) for k in range(4)])
    other = swap(total)
    total = give_call(total, other)
    total = exchange(total, PLANE)
    gx = norm_call(x, gain, wt, grad)
    pair = exchange(pair, "depth")
    gw, gpw, gpb, gb, gg, gs = finish_call(total)
    return (
        jnp.transpose(pair.reshape(64, 32, 128), (2, 0, 1)),
        gx.reshape(alignment.shape),
        gpw.T,
        gpb.reshape(64),
        gw,
        gb.reshape(128),
        gg.reshape(256),
        gs.reshape(256),
    )


def solution(mesh):
    split = Mesh(mesh.devices.reshape(4, 4, 4, 2), EVERY)
    side = P("depth", ("row", "col_0", "col_1"), None)
    block = P("row", ("col_0", "col_1"), "depth")
    return jax.shard_map(
        step,
        mesh=split,
        in_specs=(side, P(), P(), P(), P(), P(), P(), block),
        out_specs=(block, side, P(), P(), P(), P(), P(), P()),
        check_vma=False,
    )
```

profile of v0, /device:TPU:1, one launch (start us, length us, event | category | flops | bytes accessed | tf_op | source)
XLA Modules:
  0.0 148.2 jit_solution(4122757487613150026)
XLA Ops:
  0.6 5.0 %all-to-all-start.1 = ((bf16[4,16,32,128]{3,2,1,0:T(8,128)(2,1)}), bf16[4,16,32,128]{3,2,1,0:T(8,128)(2,1)S(1)}, u32[]{:S(2)}, u32[]{:S(2)}) async-start(bf16[4,16,32,128]{3,2,1,0:T(8,128)(2,1)} %bitcast.26), calls=%async_computation.1 | async-start | bytes 1048576 | tf_op jit(solution)/shard_map/all_to_all | solution.py:471
  5.6 4.5 %sides.1 = (bf16[16,16,16,128]{3,2,1,0:T(8,128)(2,1)}, bf16[16,16,128]{2,1,0:T(8,128)(2,1)}, bf16[1024,512]{1,0:T(8,128)(2,1)}) custom-call(bf16[1024,256]{1,0:T(8,128)(2,1)} %bitcast.18, f32[1,256]{1,0:T(1,128)} %bitcast.23, f32[1,256]{1,0:T(1,128)} %bitcast.27, bf16[64,256]{1,0:T(8,128)(2,1)} %bitcast.20, f32[1,64]{1,0:T(1,128)} %bitcast.28), custom_call_target="tpu_custom_call" | custom-call | flops 1600000000 | bytes 1000000 | tf_op jit(solution)/shard_map/sides/pallas_call | solution.py:82
  10.1 3.8 %all-to-all-done.1.s_ref = bf16[4,16,32,128]{3,2,1,0:T(8,128)(2,1)S(1)} async-done(((bf16[4,16,32,128]{3,2,1,0:T(8,128)(2,1)}), bf16[4,16,32,128]{3,2,1,0:T(8,128)(2,1)S(1)}, u32[]{:S(2)}, u32[]{:S(2)}) %all-to-all-start.1) | async-done | bytes 524320 | tf_op jit(solution)/shard_map/all_to_all | solution.py:471
  14.0 5.7 %all-to-all-start = ((bf16[16,16,16,128]{3,2,1,0:T(8,128)(2,1)}), bf16[16,16,16,128]{3,2,1,0:T(8,128)(2,1)S(1)}, u32[]{:S(2)}, u32[]{:S(2)}) async-start(bf16[16,16,16,128]{3,2,1,0:T(8,128)(2,1)} %get-tuple-element.32), calls=%async_computation | async-start | bytes 2097152 | tf_op jit(solution)/shard_map/all_to_all | solution.py:471
  19.7 5.8 %collective-permute-start.1 = (bf16[16,16,128]{2,1,0:T(8,128)(2,1)S(1)}, bf16[16,16,128]{2,1,0:T(8,128)(2,1)S(1)}, u32[]{:S(2)}, u32[]{:S(2)}) collective-permute-start(bf16[16,16,128]{2,1,0:T(8,128)(2,1)S(1)} %copy-done.12), channel_id=1, source_target_pairs={{0,0},{1,32},{2,64},{3,96},{4,1},{5,33},{6,65},{7,97},{8,2},{9,34}... | collective-permute-start | bytes 196616 | tf_op jit(solution)/shard_map/ppermute | solution.py:573
  25.6 12.3 %collective-permute-done.1.r0_ref = bf16[16,16,128]{2,1,0:T(8,128)(2,1)S(1)} collective-permute-done((bf16[16,16,128]{2,1,0:T(8,128)(2,1)S(1)}, bf16[16,16,128]{2,1,0:T(8,128)(2,1)S(1)}, u32[]{:S(2)}, u32[]{:S(2)}) %collective-permute-start.1) | collective-permute-done | bytes 65568 | tf_op jit(solution)/shard_map/ppermute | solution.py:573
  37.9 2.7 %collective-permute-start.4 = (bf16[16,16,128]{2,1,0:T(8,128)(2,1)S(1)}, bf16[16,16,128]{2,1,0:T(8,128)(2,1)S(1)}, u32[]{:S(2)}, u32[]{:S(2)}) collective-permute-start(bf16[16,16,128]{2,1,0:T(8,128)(2,1)S(1)} %collective-permute-done.1.r0_ref), channel_id=1, source_target_pairs={{0,24},{8,0},{16,8},{24,16},{1,25},{9,1},{17,9},{25,17},{2,26},{10... | collective-permute-start | bytes 196616 | tf_op jit(solution)/shard_map/ppermute | solution.py:492
  40.6 5.7 %grad.1 = (bf16[32,512,128]{2,1,0:T(8,128)(2,1)}, bf16[128,2048]{1,0:T(8,128)(2,1)}, f32[1,128]{1,0:T(1,128)}) custom-call(bf16[4,16,32,128]{3,2,1,0:T(8,128)(2,1)} %copy-done.7, bf16[1024,128]{1,0:T(8,128)(2,1)} %w_ref.3), custom_call_target="tpu_custom_call" | custom-call | flops 2000000000 | bytes 1000000 | tf_op jit(solution)/shard_map/grad/pallas_call | solution.py:139
  47.0 9.5 %left.1 = (bf16[16,16,16,128]{3,2,1,0:T(8,128)(2,1)}, bf16[16,16,16,128]{3,2,1,0:T(8,128)(2,1)}, bf16[512,256]{1,0:T(8,128)(2,1)}) custom-call(bf16[16,16,128]{2,1,0:T(8,128)(2,1)} %copy-done.8, bf16[16,16,128]{2,1,0:T(8,128)(2,1)} %copy-done.9, bf16[16,16,128]{2,1,0:T(8,128)(2,1)} %copy-done.10, bf16[16,16,128]{2,1,0:T(8,128)(2,1)} %copy-done.11, ...), custom_call_target="tpu_custom_call" | custom-call | flops 2000000000 | bytes 1000000 | tf_op jit(solution)/shard_map/left/pallas_call | solution.py:204
  57.1 2.4 %collective-permute-done.5 = bf16[16,16,16,128]{3,2,1,0:T(8,128)(2,1)S(1)} collective-permute-done((bf16[16,16,16,128]{3,2,1,0:T(8,128)(2,1)}, bf16[16,16,16,128]{3,2,1,0:T(8,128)(2,1)S(1)}, u32[]{:S(2)}, u32[]{:S(2)}) %collective-permute-start.5) | collective-permute-done | bytes 1048608 | tf_op jit(solution)/shard_map/ppermute | solution.py:475
  59.5 2.6 %add_convert_fusion = bf16[16,16,16,128]{3,2,1,0:T(8,128)(2,1)} fusion(bf16[16,16,16,128]{3,2,1,0:T(8,128)(2,1)S(1)} %collective-permute-done.5, bf16[16,16,16,128]{3,2,1,0:T(8,128)(2,1)} %get-tuple-element.39), kind=kLoop, calls=%fused_computation | loop fusion | flops 2097152 | bytes 3145728 | tf_op jit(solution)/shard_map/convert_element_type | solution.py:581
  62.1 7.7 %all-to-all-start.3 = ((bf16[16,16,16,128]{3,2,1,0:T(8,128)(2,1)}), bf16[16,16,16,128]{3,2,1,0:T(8,128)(2,1)S(1)}, u32[]{:S(2)}, u32[]{:S(2)}) async-start(bf16[16,16,16,128]{3,2,1,0:T(8,128)(2,1)} %add_convert_fusion), calls=%async_computation.3 | async-start | bytes 2097152 | tf_op jit(solution)/shard_map/all_to_all | solution.py:471
  69.8 5.3 %right.1 = (bf16[16,16,128]{2,1,0:T(8,128)(2,1)}, bf16[16,16,128]{2,1,0:T(8,128)(2,1)}, bf16[16,16,128]{2,1,0:T(8,128)(2,1)}, bf16[16,16,128]{2,1,0:T(8,128)(2,1)}, bf16[4096,256]{1,0:T(8,128)(2,1)}) custom-call(bf16[16,16,16,128]{3,2,1,0:T(8,128)(2,1)} %copy-done.6, bf16[16,16,16,128]{3,2,1,0:T(8,128)(2,1)} %collective-permute-done.far_ref, ...), custom_call_target="tpu_custom_call" | custom-call | flops 2000000000 | bytes 1000000 | tf_op jit(solution)/shard_map/right/pallas_call | solution.py:276
  75.1 1.2 collective-permute-start.6
  76.4 2.5 %collective-permute-start.8 = (bf16[16,16,128]{2,1,0:T(8,128)(2,1)}, bf16[16,16,128]{2,1,0:T(8,128)(2,1)S(1)}, u32[]{:S(2)}, u32[]{:S(2)}) collective-permute-start(bf16[16,16,128]{2,1,0:T(8,128)(2,1)} %get-tuple-element.44), channel_id=1, source_target_pairs={{0,24},{8,0},{16,8},{24,16},{1,25},{9,1},{17,9},{25,17},{2,26},{10... | collective-permute-start | bytes 196616 | tf_op jit(solution)/shard_map/ppermute | solution.py:492
  78.8 1.2 collective-permute-done.6
  80.0 1.5 collective-permute-done.7
  81.5 0.9 add_convert_fusion.1
  82.4 6.7 %collective-permute-start.9 = (bf16[16,16,128]{2,1,0:T(8,128)(2,1)S(1)}, bf16[16,16,128]{2,1,0:T(8,128)(2,1)S(1)}, u32[]{:S(2)}, u32[]{:S(2)}) collective-permute-start(bf16[16,16,128]{2,1,0:T(8,128)(2,1)S(1)} %add_convert_fusion.1), channel_id=1, source_target_pairs={{0,0},{32,1},{64,2},{96,3},{1,4},{33,5},{65,6},{97,7},{2,8},{34,9}... | collective-permute-start | bytes 196616 | tf_op jit(solution)/shard_map/ppermute | solution.py:588
  89.1 11.0 %outer.1 = (bf16[4,16,32,128]{3,2,1,0:T(8,128)(2,1)}, bf16[1024,128]{1,0:T(8,128)(2,1)}) custom-call(bf16[4096,256]{1,0:T(8,128)(2,1)} %get-tuple-element.34.lt_ref, bf16[512,256]{1,0:T(8,128)(2,1)} %get-tuple-element.36.rt_ref, bf16[128,2048]{1,0:T(8,128)(2,1)} %get-tuple-element.37.st_ref, bf16[1024,128]{1,0:T(8,128)(2,1)} %w_ref.3, f32[1,128]{1,0:T(1,128)} %bitcast.29), custom_call_target="tpu_custom_call" | custom-call | flops 4400000000 | bytes 1000000 | tf_op jit(solution)/shard_map/outer/pallas_call | solution.py:346
  100.2 0.9 copy-done.4
  101.8 16.3 %all_to_all.30 = bf16[16,80,128]{2,1,0:T(8,128)(2,1)S(1)} all-to-all(bf16[16,80,128]{2,1,0:T(8,128)(2,1)S(1)} %get-tuple-element.49), channel_id=1, replica_groups=mesh['depth'=4,'row'=4,'col_0'=4,'col_1'=2] {'depth','row'}, dimensions={0} | all-to-all | bytes 655360 | tf_op jit(solution)/shard_map/all_to_all | solution.py:471
  118.0 3.5 %all-to-all-start.2 = ((bf16[4,16,32,128]{3,2,1,0:T(8,128)(2,1)}), bf16[4,16,32,128]{3,2,1,0:T(8,128)(2,1)S(1)}, u32[]{:S(2)}, u32[]{:S(2)}) async-start(bf16[4,16,32,128]{3,2,1,0:T(8,128)(2,1)} %get-tuple-element.38), calls=%async_computation.2 | async-start | bytes 1048576 | tf_op jit(solution)/shard_map/all_to_all | solution.py:471
  122.3 2.2 %collective-permute-done.10 = f32[80,128]{1,0:T(8,128)S(1)} collective-permute-done((f32[80,128]{1,0:T(8,128)S(1)}, f32[80,128]{1,0:T(8,128)S(1)}, u32[]{:S(2)}, u32[]{:S(2)}) %collective-permute-start.10) | collective-permute-done | bytes 40992 | tf_op jit(solution)/shard_map/ppermute | solution.py:596
  124.5 4.3 %collective-permute-done.11 = f32[80,128]{1,0:T(8,128)S(1)} collective-permute-done((f32[80,128]{1,0:T(8,128)S(1)}, f32[80,128]{1,0:T(8,128)S(1)}, u32[]{:S(2)}, u32[]{:S(2)}) %collective-permute-start.11) | collective-permute-done | bytes 40992 | tf_op jit(solution)/shard_map/ppermute | solution.py:596
  128.9 2.4 %collective-permute-start.12 = (f32[80,128]{1,0:T(8,128)S(1)}, f32[80,128]{1,0:T(8,128)S(1)}, u32[]{:S(2)}, u32[]{:S(2)}) collective-permute-start(f32[80,128]{1,0:T(8,128)S(1)} %add.23.a_ref), channel_id=1, source_target_pairs={{0,1},{1,0},{2,3},{3,2},{4,5},{5,4},{6,7},{7,6},{8,9},{9,8},{10,11... | collective-permute-start | bytes 122888 | tf_op jit(solution)/shard_map/ppermute | solution.py:475
  131.3 0.9 collective-permute-done.12.b_ref
  132.9 4.8 %all-to-all-start.5 = ((bf16[16,80,128]{2,1,0:T(8,128)(2,1)}), bf16[16,80,128]{2,1,0:T(8,128)(2,1)S(1)}, u32[]{:S(2)}, u32[]{:S(2)}) async-start(bf16[16,80,128]{2,1,0:T(8,128)(2,1)} %give.1), calls=%async_computation.5 | async-start | bytes 655360 | tf_op jit(solution)/shard_map/all_to_all | solution.py:471
  137.8 4.8 %norm.1 = bf16[1024,256]{1,0:T(8,128)(2,1)} custom-call(bf16[1024,256]{1,0:T(8,128)(2,1)S(1)} %bitcast.19, f32[1,256]{1,0:T(1,128)S(1)} %bitcast.24, bf16[64,256]{1,0:T(8,128)(2,1)S(1)} %bitcast.22, bf16[64,1024]{1,0:T(8,128)(2,1)S(1)} %get-tuple-element.48.grad_ref), custom_call_target="tpu_custom_call" | custom-call | flops 2000000000 | bytes 1000000 | tf_op jit(solution)/shard_map/norm/pallas_call | solution.py:458
  142.6 4.1 %all-to-all-done.5.all_ref = bf16[16,80,128]{2,1,0:T(8,128)(2,1)S(1)} async-done(((bf16[16,80,128]{2,1,0:T(8,128)(2,1)}), bf16[16,80,128]{2,1,0:T(8,128)(2,1)S(1)}, u32[]{:S(2)}, u32[]{:S(2)}) %all-to-all-start.5) | async-done | bytes 327712 | tf_op jit(solution)/shard_map/all_to_all | solution.py:471
  146.6 0.8 finish.1
  147.5 0.8 copy.17
  (46 shorter events, 3.4 us)
Async XLA Ops:
  0.6 13.3 %all-to-all-start.1 = ((bf16[4,16,32,128]{3,2,1,0:T(8,128)(2,1)}), bf16[4,16,32,128]{3,2,1,0:T(8,128)(2,1)S(1)}, u32[]{:S(2)}, u32[]{:S(2)}) async-start(bf16[4,16,32,128]{3,2,1,0:T(8,128)(2,1)} %bitcast.26), calls=%async_computation.1 | async-start | bytes 1048576 | tf_op jit(solution)/shard_map/all_to_all | solution.py:471
  10.1 9.6 %copy-start.12 = (bf16[16,16,128]{2,1,0:T(8,128)(2,1)S(1)}, bf16[16,16,128]{2,1,0:T(8,128)(2,1)}, u32[]{:S(2)}) copy-start(bf16[16,16,128]{2,1,0:T(8,128)(2,1)} %get-tuple-element.35) | copy-start | bytes 196612
  14.0 26.6 %copy-start.7 = (bf16[4,16,32,128]{3,2,1,0:T(8,128)(2,1)}, bf16[4,16,32,128]{3,2,1,0:T(8,128)(2,1)S(1)}, u32[]{:S(2)}) copy-start(bf16[4,16,32,128]{3,2,1,0:T(8,128)(2,1)S(1)} %all-to-all-done.1.s_ref) | copy-start | bytes 1572868
  14.0 42.7 %all-to-all-start = ((bf16[16,16,16,128]{3,2,1,0:T(8,128)(2,1)}), bf16[16,16,16,128]{3,2,1,0:T(8,128)(2,1)S(1)}, u32[]{:S(2)}, u32[]{:S(2)}) async-start(bf16[16,16,16,128]{3,2,1,0:T(8,128)(2,1)} %get-tuple-element.32), calls=%async_computation | async-start | bytes 2097152 | tf_op jit(solution)/shard_map/all_to_all | solution.py:471
  19.7 18.2 %collective-permute-start.1 = (bf16[16,16,128]{2,1,0:T(8,128)(2,1)S(1)}, bf16[16,16,128]{2,1,0:T(8,128)(2,1)S(1)}, u32[]{:S(2)}, u32[]{:S(2)}) collective-permute-start(bf16[16,16,128]{2,1,0:T(8,128)(2,1)S(1)} %copy-done.12), channel_id=1, source_target_pairs={{0,0},{1,32},{2,64},{3,96},{4,1},{5,33},{6,65},{7,97},{8,2},{9,34}... | collective-permute-start | bytes 196616 | tf_op jit(solution)/shard_map/ppermute | solution.py:573
  37.9 8.4 %copy-start.8 = (bf16[16,16,128]{2,1,0:T(8,128)(2,1)}, bf16[16,16,128]{2,1,0:T(8,128)(2,1)S(1)}, u32[]{:S(2)}) copy-start(bf16[16,16,128]{2,1,0:T(8,128)(2,1)S(1)} %collective-permute-done.1.r0_ref) | copy-start | bytes 196612
  37.9 8.4 %collective-permute-start.2 = (bf16[16,16,128]{2,1,0:T(8,128)(2,1)S(1)}, bf16[16,16,128]{2,1,0:T(8,128)(2,1)S(1)}, u32[]{:S(2)}, u32[]{:S(2)}) collective-permute-start(bf16[16,16,128]{2,1,0:T(8,128)(2,1)S(1)} %collective-permute-done.1.r0_ref), channel_id=1, source_target_pairs={{0,8},{8,16},{16,24},{24,0},{1,9},{9,17},{17,25},{25,1},{2,10},{10... | collective-permute-start | bytes 196616 | tf_op jit(solution)/shard_map/ppermute | solution.py:492
  37.9 8.5 %collective-permute-start.3 = (bf16[16,16,128]{2,1,0:T(8,128)(2,1)S(1)}, bf16[16,16,128]{2,1,0:T(8,128)(2,1)S(1)}, u32[]{:S(2)}, u32[]{:S(2)}) collective-permute-start(bf16[16,16,128]{2,1,0:T(8,128)(2,1)S(1)} %collective-permute-done.1.r0_ref), channel_id=1, source_target_pairs={{0,16},{8,24},{16,0},{24,8},{1,17},{9,25},{17,1},{25,9},{2,18},{10... | collective-permute-start | bytes 196616 | tf_op jit(solution)/shard_map/ppermute | solution.py:492
  37.9 8.5 %collective-permute-start.4 = (bf16[16,16,128]{2,1,0:T(8,128)(2,1)S(1)}, bf16[16,16,128]{2,1,0:T(8,128)(2,1)S(1)}, u32[]{:S(2)}, u32[]{:S(2)}) collective-permute-start(bf16[16,16,128]{2,1,0:T(8,128)(2,1)S(1)} %collective-permute-done.1.r0_ref), channel_id=1, source_target_pairs={{0,24},{8,0},{16,8},{24,16},{1,25},{9,1},{17,9},{25,17},{2,26},{10... | collective-permute-start | bytes 196616 | tf_op jit(solution)/shard_map/ppermute | solution.py:492
  46.4 0.6 copy-start.9
  46.4 0.6 copy-start.10
  46.4 0.6 copy-start.11
  56.5 3.0 %collective-permute-start.5 = (bf16[16,16,16,128]{3,2,1,0:T(8,128)(2,1)}, bf16[16,16,16,128]{3,2,1,0:T(8,128)(2,1)S(1)}, u32[]{:S(2)}, u32[]{:S(2)}) collective-permute-start(bf16[16,16,16,128]{3,2,1,0:T(8,128)(2,1)} %get-tuple-element.40), channel_id=1, source_target_pairs={{0,1},{1,0},{2,3},{3,2},{4,5},{5,4},{6,7},{7,6},{8,9},{9,8},{10,11... | collective-permute-start | bytes 3145736 | tf_op jit(solution)/shard_map/ppermute | solution.py:475
  56.7 5.4 %copy-start.6 = (bf16[16,16,16,128]{3,2,1,0:T(8,128)(2,1)}, bf16[16,16,16,128]{3,2,1,0:T(8,128)(2,1)S(1)}, u32[]{:S(2)}) copy-start(bf16[16,16,16,128]{3,2,1,0:T(8,128)(2,1)S(1)} %all-to-all-done.near_ref) | copy-start | bytes 3145732
  56.7 13.1 %collective-permute-start = (bf16[16,16,16,128]{3,2,1,0:T(8,128)(2,1)S(1)}, bf16[16,16,16,128]{3,2,1,0:T(8,128)(2,1)}, u32[]{:S(2)}, u32[]{:S(2)}) collective-permute-start(bf16[16,16,16,128]{3,2,1,0:T(8,128)(2,1)S(1)} %all-to-all-done.near_ref), channel_id=1, source_target_pairs={{0,1},{1,0},{2,3},{3,2},{4,5},{5,4},{6,7},{7,6},{8,9},{9,8},{10,11... | collective-permute-start | bytes 3145736 | tf_op jit(solution)/shard_map/ppermute | solution.py:475
  62.1 38.1 %all-to-all-start.3 = ((bf16[16,16,16,128]{3,2,1,0:T(8,128)(2,1)}), bf16[16,16,16,128]{3,2,1,0:T(8,128)(2,1)S(1)}, u32[]{:S(2)}, u32[]{:S(2)}) async-start(bf16[16,16,16,128]{3,2,1,0:T(8,128)(2,1)} %add_convert_fusion), calls=%async_computation.3 | async-start | bytes 2097152 | tf_op jit(solution)/shard_map/all_to_all | solution.py:471
  75.1 4.9 %collective-permute-start.6 = (bf16[16,16,128]{2,1,0:T(8,128)(2,1)}, bf16[16,16,128]{2,1,0:T(8,128)(2,1)S(1)}, u32[]{:S(2)}, u32[]{:S(2)}) collective-permute-start(bf16[16,16,128]{2,1,0:T(8,128)(2,1)} %get-tuple-element.42), channel_id=1, source_target_pairs={{0,8},{8,16},{16,24},{24,0},{1,9},{9,17},{17,25},{25,1},{2,10},{10... | collective-permute-start | bytes 196616 | tf_op jit(solution)/shard_map/ppermute | solution.py:492
  76.4 5.1 %collective-permute-start.7 = (bf16[16,16,128]{2,1,0:T(8,128)(2,1)}, bf16[16,16,128]{2,1,0:T(8,128)(2,1)S(1)}, u32[]{:S(2)}, u32[]{:S(2)}) collective-permute-start(bf16[16,16,128]{2,1,0:T(8,128)(2,1)} %get-tuple-element.43), channel_id=1, source_target_pairs={{0,16},{8,24},{16,0},{24,8},{1,17},{9,25},{17,1},{25,9},{2,18},{10... | collective-permute-start | bytes 196616 | tf_op jit(solution)/shard_map/ppermute | solution.py:492
  76.4 5.1 %collective-permute-start.8 = (bf16[16,16,128]{2,1,0:T(8,128)(2,1)}, bf16[16,16,128]{2,1,0:T(8,128)(2,1)S(1)}, u32[]{:S(2)}, u32[]{:S(2)}) collective-permute-start(bf16[16,16,128]{2,1,0:T(8,128)(2,1)} %get-tuple-element.44), channel_id=1, source_target_pairs={{0,24},{8,0},{16,8},{24,16},{1,25},{9,1},{17,9},{25,17},{2,26},{10... | collective-permute-start | bytes 196616 | tf_op jit(solution)/shard_map/ppermute | solution.py:492
  82.4 17.8 %collective-permute-start.9 = (bf16[16,16,128]{2,1,0:T(8,128)(2,1)S(1)}, bf16[16,16,128]{2,1,0:T(8,128)(2,1)S(1)}, u32[]{:S(2)}, u32[]{:S(2)}) collective-permute-start(bf16[16,16,128]{2,1,0:T(8,128)(2,1)S(1)} %add_convert_fusion.1), channel_id=1, source_target_pairs={{0,0},{32,1},{64,2},{96,3},{1,4},{33,5},{65,6},{97,7},{2,8},{34,9}... | collective-permute-start | bytes 196616 | tf_op jit(solution)/shard_map/ppermute | solution.py:588
  89.1 11.1 %copy-start.1 = (bf16[256,64]{0,1:T(8,128)(2,1)S(1)}, bf16[256,64]{0,1:T(8,128)(2,1)}, u32[]{:S(2)}) copy-start(bf16[256,64]{0,1:T(8,128)(2,1)} %param.11) | copy-start | bytes 98308
  89.1 11.1 %copy-start.3 = (bf16[1024,512]{1,0:T(8,128)(2,1)S(1)}, bf16[1024,512]{1,0:T(8,128)(2,1)}, u32[]{:S(2)}) copy-start(bf16[1024,512]{1,0:T(8,128)(2,1)} %get-tuple-element.45.normed_ref) | copy-start | bytes 3145732
  89.1 11.1 %copy-start.5 = (f32[1,128]{1,0:T(1,128)S(1)}, f32[1,128]{1,0:T(1,128)}, u32[]{:S(2)}) copy-start(f32[1,128]{1,0:T(1,128)} %get-tuple-element.46.count_ref) | copy-start | bytes 1540
  100.2 1.0 copy-start.4
  101.8 36.0 %copy-start = (bf16[64,16,256]{2,1,0:T(8,128)(2,1)S(1)}, bf16[64,16,256]{2,1,0:T(8,128)(2,1)}, u32[]{:S(2)}) copy-start(bf16[64,16,256]{2,1,0:T(8,128)(2,1)} %param.8) | copy-start | bytes 1572868
  101.8 36.0 %copy-start.2 = (f32[256]{0:T(256)S(1)}, f32[256]{0:T(256)}, u32[]{:S(2)}) copy-start(f32[256]{0:T(256)} %param.9) | copy-start | bytes 3076
  118.0 14.9 %all-to-all-start.2 = ((bf16[4,16,32,128]{3,2,1,0:T(8,128)(2,1)}), bf16[4,16,32,128]{3,2,1,0:T(8,128)(2,1)S(1)}, u32[]{:S(2)}, u32[]{:S(2)}) async-start(bf16[4,16,32,128]{3,2,1,0:T(8,128)(2,1)} %get-tuple-element.38), calls=%async_computation.2 | async-start | bytes 1048576 | tf_op jit(solution)/shard_map/all_to_all | solution.py:471
  121.6 2.9 %collective-permute-start.10 = (f32[80,128]{1,0:T(8,128)S(1)}, f32[80,128]{1,0:T(8,128)S(1)}, u32[]{:S(2)}, u32[]{:S(2)}) collective-permute-start(f32[80,128]{1,0:T(8,128)S(1)} %convert_reduce_fusion), channel_id=1, source_target_pairs={{0,2},{2,0},{4,6},{6,4},{1,3},{3,1},{5,7},{7,5},{8,10},{10,8},{12,... | collective-permute-start | bytes 122888 | tf_op jit(solution)/shard_map/ppermute | solution.py:596
  124.5 4.4 %collective-permute-start.11 = (f32[80,128]{1,0:T(8,128)S(1)}, f32[80,128]{1,0:T(8,128)S(1)}, u32[]{:S(2)}, u32[]{:S(2)}) collective-permute-start(f32[80,128]{1,0:T(8,128)S(1)} %add.22), channel_id=1, source_target_pairs={{0,6},{2,4},{4,2},{6,0},{1,7},{3,5},{5,3},{7,1},{8,14},{10,12},{12... | collective-permute-start | bytes 122888 | tf_op jit(solution)/shard_map/ppermute | solution.py:596
  128.9 3.3 %collective-permute-start.12 = (f32[80,128]{1,0:T(8,128)S(1)}, f32[80,128]{1,0:T(8,128)S(1)}, u32[]{:S(2)}, u32[]{:S(2)}) collective-permute-start(f32[80,128]{1,0:T(8,128)S(1)} %add.23.a_ref), channel_id=1, source_target_pairs={{0,1},{1,0},{2,3},{3,2},{4,5},{5,4},{6,7},{7,6},{8,9},{9,8},{10,11... | collective-permute-start | bytes 122888 | tf_op jit(solution)/shard_map/ppermute | solution.py:475
  132.9 13.7 %all-to-all-start.5 = ((bf16[16,80,128]{2,1,0:T(8,128)(2,1)}), bf16[16,80,128]{2,1,0:T(8,128)(2,1)S(1)}, u32[]{:S(2)}, u32[]{:S(2)}) async-start(bf16[16,80,128]{2,1,0:T(8,128)(2,1)} %give.1), calls=%async_computation.5 | async-start | bytes 655360 | tf_op jit(solution)/shard_map/all_to_all | solution.py:471
where the time goes:
time: 149 us; the launch traced here: 148 us
  starting transfers between devices  49.4 us (33%)
  Pallas kernels  43 us (29%)
  waiting for transfers between devices  32.7 us (22%)
  blocking collectives  16.3 us (11%)
  other arithmetic  3.53 us (2%)
  local copies, waits for them, and re-layouts  2.41 us (2%)
    all_to_all x5, starting transfers between devices, exchange(): return lax.all_to_all(value, axis, 0, 0, tiled=True)  26.8 us
    all_to_all x1, blocking collectives, exchange(): return lax.all_to_all(value, axis, 0, 0, tiled=True)  16.3 us
    ppermute x1, waiting for transfers between devices, step(): rights = [lax.ppermute(right, EVERY, pairs)]  12.3 us
    pallas_call x1, Pallas kernels, outer_call(): pl.pallas_call(outer_kernel, out_shape=(jax.ShapeDtypeStruct((4, 16, 32,...  11 us
    pallas_call x1, Pallas kernels, left_call(): pl.pallas_call(left_kernel, out_shape=(jax.ShapeDtypeStruct((16, 16, 16,...  9.51 us
    all_to_all x5, waiting for transfers between devices, exchange(): return lax.all_to_all(value, axis, 0, 0, tiled=True)  7.9 us
    ppermute x1, starting transfers between devices, step(): right_grad = lax.ppermute(right_grad, EVERY, [(b, a) for a, b in pairs])  6.73 us
    ppermute x2, waiting for transfers between devices, step(): total = total + lax.ppermute(total, 'col_0', [(k, k ^ m) for k in range(4)])  6.58 us
  transfers between devices with their start and end apart: 18, of which 9 were waited for; matrix products, arithmetic and copies ran while one was open for 2% of the time, Pallas kernels for 28%

commit v1 on v0

--- a/solution.py
+++ b/solution.py
@@ -295,8 +295,11 @@
 
 
 def outer_kernel(
-    lt_ref, rt_ref, st_ref, w_ref, bias_ref, pair_ref, gw_ref, tall, xs, lt, sems
+    lt_ref, rt_ref, st_ref, w_ref, bias_ref,
+    p0_ref, p1_ref, p2_ref, p3_ref, gw_ref,
+    tall, xs, lt, sems, pair,
 ):
+    depth = lax.axis_index("depth")
     copies = []
     for q in range(4):
         part = pl.ds(q * 1024, 1024)
@@ -332,7 +335,11 @@
         part = (part * (1.0 / 256) + bias).astype(BF16)
         for jj in range(2):
             for d in range(4):
-                pair_ref[d, j + jj] = part[d * 32 : (d + 1) * 32, jj * 128 : (jj + 1) * 128]
+                pair[lax.rem(d - depth + 4, 4), j + jj] = part[
+                    d * 32 : (d + 1) * 32, jj * 128 : (jj + 1) * 128
+                ]
+    for m, ref in enumerate((p0_ref, p1_ref, p2_ref, p3_ref)):
+        ref[...] = pair[m]
 
     def weight(k, _):
         at = pl.multiple_of(k * 256, 256)
@@ -346,16 +353,17 @@
     return pl.pallas_call(
         outer_kernel,
         out_shape=(
-            jax.ShapeDtypeStruct((4, 16, 32, 128), BF16),
+            *[jax.ShapeDtypeStruct((16, 32, 128), BF16)] * 4,
             jax.ShapeDtypeStruct((1024, 128), BF16),
         ),
         in_specs=(*hbm(1), *vmem(4)),
-        out_specs=tuple(vmem(2)),
+        out_specs=tuple(vmem(5)),
         scratch_shapes=[
             pltpu.VMEM((128, 128, 128), F32),
             pltpu.VMEM((1024, 2048), BF16),
             pltpu.VMEM((4096, 256), BF16),
             pltpu.SemaphoreType.DMA((4,)),
+            pltpu.VMEM((4, 16, 32, 128), BF16),
         ],
         cost_estimate=cost(11),
         name="outer",
@@ -421,8 +429,15 @@
     )(gl, gr, normed, wt, count, gw)
 
 
-def norm_kernel(x_ref, gain_ref, wt_ref, grad_ref, gx_ref, rows, rstds):
+def norm_kernel(
+    x_ref, gain_ref, wt_ref, grad_ref, p0_ref, p1_ref, p2_ref, p3_ref,
+    gx_ref, pair_ref,
+    rows, rstds,
+):
     seqs, own = 64, 16
+    depth = lax.axis_index("depth")
+    for m, ref in enumerate((p0_ref, p1_ref, p2_ref, p3_ref)):
+        pair_ref[pl.ds(lax.rem(depth - m + 4, 4) * 16, 16)] = ref[...]
     gain = gain_ref[...]
 
     def block(k, _):
@@ -454,17 +469,20 @@
         gx_ref[:, h * 128 : (h + 1) * 128] = rows[h].astype(BF16)
 
 
-def norm_call(x, gain, wt, grad):
+def norm_call(x, gain, wt, grad, pair):
     return pl.pallas_call(
         norm_kernel,
-        out_shape=jax.ShapeDtypeStruct((1024, 256), BF16),
-        in_specs=vmem(4),
-        out_specs=pl.BlockSpec(memory_space=pltpu.VMEM),
+        out_shape=(
+            jax.ShapeDtypeStruct((1024, 256), BF16),
+            jax.ShapeDtypeStruct((64, 32, 128), BF16),
+        ),
+        in_specs=vmem(8),
+        out_specs=tuple(vmem(2)),
         scratch_shapes=[pltpu.VMEM((2, 1024, 128), F32), pltpu.VMEM((1024, 128), F32)],
-        compiler_params=limit(8),
+        compiler_params=limit(10),
         cost_estimate=cost(5),
         name="norm",
-    )(x, gain, wt, grad)
+    )(x, gain, wt, grad, *pair)
 
 
 def exchange(value, axis):
@@ -587,7 +605,7 @@
     right_grad = sum(g.astype(F32) for g in gr).astype(BF16)
     right_grad = lax.ppermute(right_grad, EVERY, [(b, a) for a, b in pairs])
 
-    pair, gw = outer_call(lt, rt, st, out_weight, out_bias.reshape(1, 128))
+    *pair, gw = outer_call(lt, rt, st, out_weight, out_bias.reshape(1, 128))
     grad, total = back_call(lefts, right_grad, normed, wt, count, gw)
 
     total = exchange(total, PLANE)
@@ -597,11 +615,12 @@
     other = swap(total)
     total = give_call(total, other)
     total = exchange(total, PLANE)
-    gx = norm_call(x, gain, wt, grad)
-    pair = exchange(pair, "depth")
+    for m in range(1, 4):
+        pair[m] = rotate(pair[m], "depth", m)
+    gx, pair = norm_call(x, gain, wt, grad, pair)
     gw, gpw, gpb, gb, gg, gs = finish_call(total)
     return (
-        jnp.transpose(pair.reshape(64, 32, 128), (2, 0, 1)),
+        jnp.transpose(pair, (2, 0, 1)),
         gx.reshape(alignment.shape),
         gpw.T,
         gpb.reshape(64),

time: 149 us -> 147 us (0.987)
  waiting for transfers between devices: 32.7 us -> 30.9 us
    all_to_all x5 -> x4, starting transfers between devices: 26.8 us -> 22.4 us  [exchange(): return lax.all_to_all(value, axis, 0, 0, tiled=True)]
    ppermute x6 -> x9, starting transfers between devices: 6.41 us -> 9.16 us  [rotate(): return lax.ppermute(value, axis, [(k, (k + by) % 4) for k in range(4)])]
    all_to_all x5 -> x4, waiting for transfers between devices: 7.9 us -> 5.39 us  [exchange(): return lax.all_to_all(value, axis, 0, 0, tiled=True)]
    ppermute x6 -> x9, waiting for transfers between devices: 2.65 us -> 4.55 us  [rotate(): return lax.ppermute(value, axis, [(k, (k + by) % 4) for k in range(4)])]
  transfers between devices with their start and end apart: 18 -> 20, of which waited for: 9 -> 10; matrix products, arithmetic and copies ran while one was open for 2% -> 2% of each run, Pallas kernels for 28% -> 29%
where the time goes in v1:
time: 147 us; the launch traced here: 145 us
  starting transfers between devices  48 us (33%)
  Pallas kernels  43.2 us (29%)
  waiting for transfers between devices  30.9 us (21%)
  blocking collectives  16.3 us (11%)
  other arithmetic  3.49 us (2%)
  local copies, waits for them, and re-layouts  2.58 us (2%)
    all_to_all x4, starting transfers between devices, exchange(): return lax.all_to_all(value, axis, 0, 0, tiled=True)  22.4 us
    all_to_all x1, blocking collectives, exchange(): return lax.all_to_all(value, axis, 0, 0, tiled=True)  16.3 us
    ppermute x1, waiting for transfers between devices, step(): rights = [lax.ppermute(right, EVERY, pairs)]  12.3 us
    pallas_call x1, Pallas kernels, outer_call(): pl.pallas_call(outer_kernel, out_shape=(*[jax.ShapeDtypeStruct((16, 32, 1...  11.1 us
    pallas_call x1, Pallas kernels, left_call(): pl.pallas_call(left_kernel, out_shape=(jax.ShapeDtypeStruct((16, 16, 16,...  9.58 us
    ppermute x9, starting transfers between devices, rotate(): return lax.ppermute(value, axis, [(k, (k + by) % 4) for k in range(4)])  9.16 us
    ppermute x1, starting transfers between devices, step(): right_grad = lax.ppermute(right_grad, EVERY, [(b, a) for a, b in pairs])  6.73 us
    ppermute x2, waiting for transfers between devices, step(): total = total + lax.ppermute(total, 'col_0', [(k, k ^ m) for k in range(4)])  6.3 us
  transfers between devices with their start and end apart: 20, of which 10 were waited for; matrix products, arithmetic and copies ran while one was open for 2% of the time, Pallas kernels for 29%

profile of v1, /device:TPU:1, one launch (start us, length us, event | category | flops | bytes accessed | tf_op | source)
XLA Modules:
  0.0 145.4 jit_solution(15508131307820706319)
XLA Ops:
  0.6 5.0 %all-to-all-start = ((bf16[4,16,32,128]{3,2,1,0:T(8,128)(2,1)}), bf16[4,16,32,128]{3,2,1,0:T(8,128)(2,1)S(1)}, u32[]{:S(2)}, u32[]{:S(2)}) async-start(bf16[4,16,32,128]{3,2,1,0:T(8,128)(2,1)} %bitcast.23), calls=%async_computation | async-start | bytes 1048576 | tf_op jit(solution)/shard_map/all_to_all | solution.py:489
  5.6 4.5 %sides.1 = (bf16[16,16,16,128]{3,2,1,0:T(8,128)(2,1)}, bf16[16,16,128]{2,1,0:T(8,128)(2,1)}, bf16[1024,512]{1,0:T(8,128)(2,1)}) custom-call(bf16[1024,256]{1,0:T(8,128)(2,1)} %bitcast.16, f32[1,256]{1,0:T(1,128)} %bitcast.21, f32[1,256]{1,0:T(1,128)} %bitcast.24, bf16[64,256]{1,0:T(8,128)(2,1)} %bitcast.18, f32[1,64]{1,0:T(1,128)} %bitcast.25), custom_call_target="tpu_custom_call" | custom-call | flops 1600000000 | bytes 1000000 | tf_op jit(solution)/shard_map/sides/pallas_call | solution.py:82
  10.1 3.8 %all-to-all-done.s_ref = bf16[4,16,32,128]{3,2,1,0:T(8,128)(2,1)S(1)} async-done(((bf16[4,16,32,128]{3,2,1,0:T(8,128)(2,1)}), bf16[4,16,32,128]{3,2,1,0:T(8,128)(2,1)S(1)}, u32[]{:S(2)}, u32[]{:S(2)}) %all-to-all-start) | async-done | bytes 524320 | tf_op jit(solution)/shard_map/all_to_all | solution.py:489
  14.0 5.7 %all-to-all-start.2 = ((bf16[16,16,16,128]{3,2,1,0:T(8,128)(2,1)}), bf16[16,16,16,128]{3,2,1,0:T(8,128)(2,1)S(1)}, u32[]{:S(2)}, u32[]{:S(2)}) async-start(bf16[16,16,16,128]{3,2,1,0:T(8,128)(2,1)} %get-tuple-element.41), calls=%async_computation.2 | async-start | bytes 2097152 | tf_op jit(solution)/shard_map/all_to_all | solution.py:489
  19.7 5.8 %collective-permute-start = (bf16[16,16,128]{2,1,0:T(8,128)(2,1)S(1)}, bf16[16,16,128]{2,1,0:T(8,128)(2,1)S(1)}, u32[]{:S(2)}, u32[]{:S(2)}) collective-permute-start(bf16[16,16,128]{2,1,0:T(8,128)(2,1)S(1)} %copy-done.17), channel_id=1, source_target_pairs={{0,0},{1,32},{2,64},{3,96},{4,1},{5,33},{6,65},{7,97},{8,2},{9,34}... | collective-permute-start | bytes 196616 | tf_op jit(solution)/shard_map/ppermute | solution.py:591
  25.6 12.3 %collective-permute-done.r0_ref = bf16[16,16,128]{2,1,0:T(8,128)(2,1)S(1)} collective-permute-done((bf16[16,16,128]{2,1,0:T(8,128)(2,1)S(1)}, bf16[16,16,128]{2,1,0:T(8,128)(2,1)S(1)}, u32[]{:S(2)}, u32[]{:S(2)}) %collective-permute-start) | collective-permute-done | bytes 65568 | tf_op jit(solution)/shard_map/ppermute | solution.py:591
  37.9 2.7 %collective-permute-start.3 = (bf16[16,16,128]{2,1,0:T(8,128)(2,1)S(1)}, bf16[16,16,128]{2,1,0:T(8,128)(2,1)S(1)}, u32[]{:S(2)}, u32[]{:S(2)}) collective-permute-start(bf16[16,16,128]{2,1,0:T(8,128)(2,1)S(1)} %collective-permute-done.r0_ref), channel_id=1, source_target_pairs={{0,24},{8,0},{16,8},{24,16},{1,25},{9,1},{17,9},{25,17},{2,26},{10... | collective-permute-start | bytes 196616 | tf_op jit(solution)/shard_map/ppermute | solution.py:510
  40.6 5.7 %grad.1 = (bf16[32,512,128]{2,1,0:T(8,128)(2,1)}, bf16[128,2048]{1,0:T(8,128)(2,1)}, f32[1,128]{1,0:T(1,128)}) custom-call(bf16[4,16,32,128]{3,2,1,0:T(8,128)(2,1)} %copy-done.8, bf16[1024,128]{1,0:T(8,128)(2,1)} %w_ref.3), custom_call_target="tpu_custom_call" | custom-call | flops 2000000000 | bytes 1000000 | tf_op jit(solution)/shard_map/grad/pallas_call | solution.py:139
  47.0 9.6 %left.1 = (bf16[16,16,16,128]{3,2,1,0:T(8,128)(2,1)}, bf16[16,16,16,128]{3,2,1,0:T(8,128)(2,1)}, bf16[512,256]{1,0:T(8,128)(2,1)}) custom-call(bf16[16,16,128]{2,1,0:T(8,128)(2,1)} %copy-done.13, bf16[16,16,128]{2,1,0:T(8,128)(2,1)} %copy-done.14, bf16[16,16,128]{2,1,0:T(8,128)(2,1)} %copy-done.15, bf16[16,16,128]{2,1,0:T(8,128)(2,1)} %copy-done.16, ...), custom_call_target="tpu_custom_call" | custom-call | flops 2000000000 | bytes 1000000 | tf_op jit(solution)/shard_map/left/pallas_call | solution.py:204
  57.2 2.4 %collective-permute-done.4 = bf16[16,16,16,128]{3,2,1,0:T(8,128)(2,1)S(1)} collective-permute-done((bf16[16,16,16,128]{3,2,1,0:T(8,128)(2,1)}, bf16[16,16,16,128]{3,2,1,0:T(8,128)(2,1)S(1)}, u32[]{:S(2)}, u32[]{:S(2)}) %collective-permute-start.4) | collective-permute-done | bytes 1048608 | tf_op jit(solution)/shard_map/ppermute | solution.py:493
  59.5 2.5 %add_convert_fusion = bf16[16,16,16,128]{3,2,1,0:T(8,128)(2,1)} fusion(bf16[16,16,16,128]{3,2,1,0:T(8,128)(2,1)S(1)} %collective-permute-done.4, bf16[16,16,16,128]{3,2,1,0:T(8,128)(2,1)} %get-tuple-element.39), kind=kLoop, calls=%fused_computation | loop fusion | flops 2097152 | bytes 3145728 | tf_op jit(solution)/shard_map/convert_element_type | solution.py:599
  62.1 7.7 %all-to-all-start.1 = ((bf16[16,16,16,128]{3,2,1,0:T(8,128)(2,1)}), bf16[16,16,16,128]{3,2,1,0:T(8,128)(2,1)S(1)}, u32[]{:S(2)}, u32[]{:S(2)}) async-start(bf16[16,16,16,128]{3,2,1,0:T(8,128)(2,1)} %add_convert_fusion), calls=%async_computation.1 | async-start | bytes 2097152 | tf_op jit(solution)/shard_map/all_to_all | solution.py:489
  69.8 1.0 copy-done.9
  70.8 5.3 %right.1 = (bf16[16,16,128]{2,1,0:T(8,128)(2,1)}, bf16[16,16,128]{2,1,0:T(8,128)(2,1)}, bf16[16,16,128]{2,1,0:T(8,128)(2,1)}, bf16[16,16,128]{2,1,0:T(8,128)(2,1)}, bf16[4096,256]{1,0:T(8,128)(2,1)}) custom-call(bf16[16,16,16,128]{3,2,1,0:T(8,128)(2,1)} %copy-done.7, bf16[16,16,16,128]{3,2,1,0:T(8,128)(2,1)} %copy-done.9, ...), custom_call_target="tpu_custom_call" | custom-call | flops 2000000000 | bytes 1000000 | tf_op jit(solution)/shard_map/right/pallas_call | solution.py:276
  76.1 1.3 collective-permute-start.6
  77.3 2.5 %collective-permute-start.8 = (bf16[16,16,128]{2,1,0:T(8,128)(2,1)}, bf16[16,16,128]{2,1,0:T(8,128)(2,1)S(1)}, u32[]{:S(2)}, u32[]{:S(2)}) collective-permute-start(bf16[16,16,128]{2,1,0:T(8,128)(2,1)} %get-tuple-element.45), channel_id=1, source_target_pairs={{0,24},{8,0},{16,8},{24,16},{1,25},{9,1},{17,9},{25,17},{2,26},{10... | collective-permute-start | bytes 196616 | tf_op jit(solution)/shard_map/ppermute | solution.py:510
  79.8 1.2 collective-permute-done.6
  81.0 1.5 %collective-permute-done.7 = bf16[16,16,128]{2,1,0:T(8,128)(2,1)S(1)} collective-permute-done((bf16[16,16,128]{2,1,0:T(8,128)(2,1)}, bf16[16,16,128]{2,1,0:T(8,128)(2,1)S(1)}, u32[]{:S(2)}, u32[]{:S(2)}) %collective-permute-start.7) | collective-permute-done | bytes 65568 | tf_op jit(solution)/shard_map/ppermute | solution.py:510
  82.4 0.9 add_convert_fusion.1
  83.3 6.7 %collective-permute-start.9 = (bf16[16,16,128]{2,1,0:T(8,128)(2,1)S(1)}, bf16[16,16,128]{2,1,0:T(8,128)(2,1)S(1)}, u32[]{:S(2)}, u32[]{:S(2)}) collective-permute-start(bf16[16,16,128]{2,1,0:T(8,128)(2,1)S(1)} %add_convert_fusion.1), channel_id=1, source_target_pairs={{0,0},{32,1},{64,2},{96,3},{1,4},{33,5},{65,6},{97,7},{2,8},{34,9}... | collective-permute-start | bytes 196616 | tf_op jit(solution)/shard_map/ppermute | solution.py:606
  90.1 11.1 %outer.1 = (bf16[16,32,128]{2,1,0:T(8,128)(2,1)}, bf16[16,32,128]{2,1,0:T(8,128)(2,1)}, bf16[16,32,128]{2,1,0:T(8,128)(2,1)}, bf16[16,32,128]{2,1,0:T(8,128)(2,1)}, bf16[1024,128]{1,0:T(8,128)(2,1)}) custom-call(bf16[4096,256]{1,0:T(8,128)(2,1)} %get-tuple-element.48.lt_ref, bf16[512,256]{1,0:T(8,128)(2,1)} %get-tuple-element.49.rt_ref, ...), custom_call_target="tpu_custom_call" | custom-call | flops 4400000000 | bytes 1000000 | tf_op jit(solution)/shard_map/outer/pallas_call | solution.py:353
  101.3 0.9 copy-done.4
  102.8 16.3 %all_to_all.25 = bf16[16,80,128]{2,1,0:T(8,128)(2,1)S(1)} all-to-all(bf16[16,80,128]{2,1,0:T(8,128)(2,1)S(1)} %get-tuple-element.59), channel_id=1, replica_groups=mesh['depth'=4,'row'=4,'col_0'=4,'col_1'=2] {'depth','row'}, dimensions={0} | all-to-all | bytes 655360 | tf_op jit(solution)/shard_map/all_to_all | solution.py:489
  119.8 2.2 %collective-permute-done.13 = f32[80,128]{1,0:T(8,128)S(1)} collective-permute-done((f32[80,128]{1,0:T(8,128)S(1)}, f32[80,128]{1,0:T(8,128)S(1)}, u32[]{:S(2)}, u32[]{:S(2)}) %collective-permute-start.13) | collective-permute-done | bytes 40992 | tf_op jit(solution)/shard_map/ppermute | solution.py:614
  122.1 4.1 %collective-permute-done.14 = f32[80,128]{1,0:T(8,128)S(1)} collective-permute-done((f32[80,128]{1,0:T(8,128)S(1)}, f32[80,128]{1,0:T(8,128)S(1)}, u32[]{:S(2)}, u32[]{:S(2)}) %collective-permute-start.14) | collective-permute-done | bytes 40992 | tf_op jit(solution)/shard_map/ppermute | solution.py:614
  126.2 2.7 %collective-permute-start.15 = (f32[80,128]{1,0:T(8,128)S(1)}, f32[80,128]{1,0:T(8,128)S(1)}, u32[]{:S(2)}, u32[]{:S(2)}) collective-permute-start(f32[80,128]{1,0:T(8,128)S(1)} %add.23.a_ref), channel_id=1, source_target_pairs={{0,1},{1,0},{2,3},{3,2},{4,5},{5,4},{6,7},{7,6},{8,9},{9,8},{10,11... | collective-permute-start | bytes 122888 | tf_op jit(solution)/shard_map/ppermute | solution.py:493
  128.9 1.8 %collective-permute-start.11 = (bf16[16,32,128]{2,1,0:T(8,128)(2,1)S(1)}, bf16[16,32,128]{2,1,0:T(8,128)(2,1)S(1)}, u32[]{:S(2)}, u32[]{:S(2)}) collective-permute-start(bf16[16,32,128]{2,1,0:T(8,128)(2,1)S(1)} %copy-done.11), channel_id=1, source_target_pairs={{0,64},{32,96},{64,0},{96,32},{1,65},{33,97},{65,1},{97,33},{2,66}... | collective-permute-start | bytes 393224 | tf_op jit(solution)/shard_map/ppermute | solution.py:510
  130.6 1.0 collective-permute-start.12
  132.4 3.9 %all-to-all-start.4 = ((bf16[16,80,128]{2,1,0:T(8,128)(2,1)}), bf16[16,80,128]{2,1,0:T(8,128)(2,1)S(1)}, u32[]{:S(2)}, u32[]{:S(2)}) async-start(bf16[16,80,128]{2,1,0:T(8,128)(2,1)} %give.1), calls=%async_computation.4 | async-start | bytes 655360 | tf_op jit(solution)/shard_map/all_to_all | solution.py:489
  136.3 1.6 %collective-permute-done.10.p1_ref = bf16[16,32,128]{2,1,0:T(8,128)(2,1)S(1)} collective-permute-done((bf16[16,32,128]{2,1,0:T(8,128)(2,1)S(1)}, bf16[16,32,128]{2,1,0:T(8,128)(2,1)S(1)}, u32[]{:S(2)}, u32[]{:S(2)}) %collective-permute-start.10) | collective-permute-done | bytes 131104 | tf_op jit(solution)/shard_map/ppermute | solution.py:510
  138.2 4.8 %norm.1 = (bf16[1024,256]{1,0:T(8,128)(2,1)}, bf16[64,32,128]{2,1,0:T(8,128)(2,1)}) custom-call(bf16[1024,256]{1,0:T(8,128)(2,1)S(1)} %bitcast.17, f32[1,256]{1,0:T(1,128)S(1)} %bitcast.22, bf16[64,256]{1,0:T(8,128)(2,1)S(1)} %bitcast.20, bf16[64,1024]{1,0:T(8,128)(2,1)S(1)} %get-tuple-element.52.grad_ref, bf16[16,32,128]{2,1,0:T(8,128)(2,1)S(1)} %copy-done.5, ...), custom_call_target="tpu_custom_call" | custom-call | flops 2000000000 | bytes 1000000 | tf_op jit(solution)/shard_map/norm/pallas_call | solution.py:473
  143.0 1.5 %all-to-all-done.4.all_ref = bf16[16,80,128]{2,1,0:T(8,128)(2,1)S(1)} async-done(((bf16[16,80,128]{2,1,0:T(8,128)(2,1)}), bf16[16,80,128]{2,1,0:T(8,128)(2,1)S(1)}, u32[]{:S(2)}, u32[]{:S(2)}) %all-to-all-start.4) | async-done | bytes 327712 | tf_op jit(solution)/shard_map/all_to_all | solution.py:489
  (59 shorter events, 4.6 us)
Async XLA Ops:
  0.6 13.3 %all-to-all-start = ((bf16[4,16,32,128]{3,2,1,0:T(8,128)(2,1)}), bf16[4,16,32,128]{3,2,1,0:T(8,128)(2,1)S(1)}, u32[]{:S(2)}, u32[]{:S(2)}) async-start(bf16[4,16,32,128]{3,2,1,0:T(8,128)(2,1)} %bitcast.23), calls=%async_computation | async-start | bytes 1048576 | tf_op jit(solution)/shard_map/all_to_all | solution.py:489
  10.1 9.6 %copy-start.17 = (bf16[16,16,128]{2,1,0:T(8,128)(2,1)S(1)}, bf16[16,16,128]{2,1,0:T(8,128)(2,1)}, u32[]{:S(2)}) copy-start(bf16[16,16,128]{2,1,0:T(8,128)(2,1)} %get-tuple-element.37) | copy-start | bytes 196612
  14.0 26.6 %copy-start.8 = (bf16[4,16,32,128]{3,2,1,0:T(8,128)(2,1)}, bf16[4,16,32,128]{3,2,1,0:T(8,128)(2,1)S(1)}, u32[]{:S(2)}) copy-start(bf16[4,16,32,128]{3,2,1,0:T(8,128)(2,1)S(1)} %all-to-all-done.s_ref) | copy-start | bytes 1572868
  14.0 42.7 %all-to-all-start.2 = ((bf16[16,16,16,128]{3,2,1,0:T(8,128)(2,1)}), bf16[16,16,16,128]{3,2,1,0:T(8,128)(2,1)S(1)}, u32[]{:S(2)}, u32[]{:S(2)}) async-start(bf16[16,16,16,128]{3,2,1,0:T(8,128)(2,1)} %get-tuple-element.41), calls=%async_computation.2 | async-start | bytes 2097152 | tf_op jit(solution)/shard_map/all_to_all | solution.py:489
  19.7 18.2 %collective-permute-start = (bf16[16,16,128]{2,1,0:T(8,128)(2,1)S(1)}, bf16[16,16,128]{2,1,0:T(8,128)(2,1)S(1)}, u32[]{:S(2)}, u32[]{:S(2)}) collective-permute-start(bf16[16,16,128]{2,1,0:T(8,128)(2,1)S(1)} %copy-done.17), channel_id=1, source_target_pairs={{0,0},{1,32},{2,64},{3,96},{4,1},{5,33},{6,65},{7,97},{8,2},{9,34}... | collective-permute-start | bytes 196616 | tf_op jit(solution)/shard_map/ppermute | solution.py:591
  37.9 8.4 %copy-start.13 = (bf16[16,16,128]{2,1,0:T(8,128)(2,1)}, bf16[16,16,128]{2,1,0:T(8,128)(2,1)S(1)}, u32[]{:S(2)}) copy-start(bf16[16,16,128]{2,1,0:T(8,128)(2,1)S(1)} %collective-permute-done.r0_ref) | copy-start | bytes 196612
  37.9 8.4 %collective-permute-start.1 = (bf16[16,16,128]{2,1,0:T(8,128)(2,1)S(1)}, bf16[16,16,128]{2,1,0:T(8,128)(2,1)S(1)}, u32[]{:S(2)}, u32[]{:S(2)}) collective-permute-start(bf16[16,16,128]{2,1,0:T(8,128)(2,1)S(1)} %collective-permute-done.r0_ref), channel_id=1, source_target_pairs={{0,8},{8,16},{16,24},{24,0},{1,9},{9,17},{17,25},{25,1},{2,10},{10... | collective-permute-start | bytes 196616 | tf_op jit(solution)/shard_map/ppermute | solution.py:510
  37.9 8.4 %collective-permute-start.2 = (bf16[16,16,128]{2,1,0:T(8,128)(2,1)S(1)}, bf16[16,16,128]{2,1,0:T(8,128)(2,1)S(1)}, u32[]{:S(2)}, u32[]{:S(2)}) collective-permute-start(bf16[16,16,128]{2,1,0:T(8,128)(2,1)S(1)} %collective-permute-done.r0_ref), channel_id=1, source_target_pairs={{0,16},{8,24},{16,0},{24,8},{1,17},{9,25},{17,1},{25,9},{2,18},{10... | collective-permute-start | bytes 196616 | tf_op jit(solution)/shard_map/ppermute | solution.py:510
  37.9 8.5 %collective-permute-start.3 = (bf16[16,16,128]{2,1,0:T(8,128)(2,1)S(1)}, bf16[16,16,128]{2,1,0:T(8,128)(2,1)S(1)}, u32[]{:S(2)}, u32[]{:S(2)}) collective-permute-start(bf16[16,16,128]{2,1,0:T(8,128)(2,1)S(1)} %collective-permute-done.r0_ref), channel_id=1, source_target_pairs={{0,24},{8,0},{16,8},{24,16},{1,25},{9,1},{17,9},{25,17},{2,26},{10... | collective-permute-start | bytes 196616 | tf_op jit(solution)/shard_map/ppermute | solution.py:510
  56.6 3.0 %collective-permute-start.4 = (bf16[16,16,16,128]{3,2,1,0:T(8,128)(2,1)}, bf16[16,16,16,128]{3,2,1,0:T(8,128)(2,1)S(1)}, u32[]{:S(2)}, u32[]{:S(2)}) collective-permute-start(bf16[16,16,16,128]{3,2,1,0:T(8,128)(2,1)} %get-tuple-element.40), channel_id=1, source_target_pairs={{0,1},{1,0},{2,3},{3,2},{4,5},{5,4},{6,7},{7,6},{8,9},{9,8},{10,11... | collective-permute-start | bytes 3145736 | tf_op jit(solution)/shard_map/ppermute | solution.py:493
  56.7 13.1 %collective-permute-start.5 = (bf16[16,16,16,128]{3,2,1,0:T(8,128)(2,1)S(1)}, bf16[16,16,16,128]{3,2,1,0:T(8,128)(2,1)S(1)}, u32[]{:S(2)}, u32[]{:S(2)}) collective-permute-start(bf16[16,16,16,128]{3,2,1,0:T(8,128)(2,1)S(1)} %all-to-all-done.2.near_ref), channel_id=1, source_target_pairs={{0,1},{1,0},{2,3},{3,2},{4,5},{5,4},{6,7},{7,6},{8,9},{9,8},{10,11... | collective-permute-start | bytes 3145736 | tf_op jit(solution)/shard_map/ppermute | solution.py:493
  62.1 39.1 %all-to-all-start.1 = ((bf16[16,16,16,128]{3,2,1,0:T(8,128)(2,1)}), bf16[16,16,16,128]{3,2,1,0:T(8,128)(2,1)S(1)}, u32[]{:S(2)}, u32[]{:S(2)}) async-start(bf16[16,16,16,128]{3,2,1,0:T(8,128)(2,1)} %add_convert_fusion), calls=%async_computation.1 | async-start | bytes 2097152 | tf_op jit(solution)/shard_map/all_to_all | solution.py:489
  76.1 4.9 %collective-permute-start.6 = (bf16[16,16,128]{2,1,0:T(8,128)(2,1)}, bf16[16,16,128]{2,1,0:T(8,128)(2,1)S(1)}, u32[]{:S(2)}, u32[]{:S(2)}) collective-permute-start(bf16[16,16,128]{2,1,0:T(8,128)(2,1)} %get-tuple-element.43), channel_id=1, source_target_pairs={{0,8},{8,16},{16,24},{24,0},{1,9},{9,17},{17,25},{25,1},{2,10},{10... | collective-permute-start | bytes 196616 | tf_op jit(solution)/shard_map/ppermute | solution.py:510
  77.3 5.1 %collective-permute-start.7 = (bf16[16,16,128]{2,1,0:T(8,128)(2,1)}, bf16[16,16,128]{2,1,0:T(8,128)(2,1)S(1)}, u32[]{:S(2)}, u32[]{:S(2)}) collective-permute-start(bf16[16,16,128]{2,1,0:T(8,128)(2,1)} %get-tuple-element.44), channel_id=1, source_target_pairs={{0,16},{8,24},{16,0},{24,8},{1,17},{9,25},{17,1},{25,9},{2,18},{10... | collective-permute-start | bytes 196616 | tf_op jit(solution)/shard_map/ppermute | solution.py:510
  77.3 5.1 %collective-permute-start.8 = (bf16[16,16,128]{2,1,0:T(8,128)(2,1)}, bf16[16,16,128]{2,1,0:T(8,128)(2,1)S(1)}, u32[]{:S(2)}, u32[]{:S(2)}) collective-permute-start(bf16[16,16,128]{2,1,0:T(8,128)(2,1)} %get-tuple-element.45), channel_id=1, source_target_pairs={{0,24},{8,0},{16,8},{24,16},{1,25},{9,1},{17,9},{25,17},{2,26},{10... | collective-permute-start | bytes 196616 | tf_op jit(solution)/shard_map/ppermute | solution.py:510
  83.3 17.9 %collective-permute-start.9 = (bf16[16,16,128]{2,1,0:T(8,128)(2,1)S(1)}, bf16[16,16,128]{2,1,0:T(8,128)(2,1)S(1)}, u32[]{:S(2)}, u32[]{:S(2)}) collective-permute-start(bf16[16,16,128]{2,1,0:T(8,128)(2,1)S(1)} %add_convert_fusion.1), channel_id=1, source_target_pairs={{0,0},{32,1},{64,2},{96,3},{1,4},{33,5},{65,6},{97,7},{2,8},{34,9}... | collective-permute-start | bytes 196616 | tf_op jit(solution)/shard_map/ppermute | solution.py:606
  90.1 11.2 %copy-start.1 = (bf16[256,64]{0,1:T(8,128)(2,1)S(1)}, bf16[256,64]{0,1:T(8,128)(2,1)}, u32[]{:S(2)}) copy-start(bf16[256,64]{0,1:T(8,128)(2,1)} %param.11) | copy-start | bytes 98308
  90.1 11.2 %copy-start.3 = (bf16[1024,512]{1,0:T(8,128)(2,1)S(1)}, bf16[1024,512]{1,0:T(8,128)(2,1)}, u32[]{:S(2)}) copy-start(bf16[1024,512]{1,0:T(8,128)(2,1)} %get-tuple-element.46.normed_ref) | copy-start | bytes 3145732
  90.1 11.2 %copy-start.6 = (f32[1,128]{1,0:T(1,128)S(1)}, f32[1,128]{1,0:T(1,128)}, u32[]{:S(2)}) copy-start(f32[1,128]{1,0:T(1,128)} %get-tuple-element.47.count_ref) | copy-start | bytes 1540
  102.2 26.6 %copy-start.12 = (bf16[16,32,128]{2,1,0:T(8,128)(2,1)S(1)}, bf16[16,32,128]{2,1,0:T(8,128)(2,1)}, u32[]{:S(2)}) copy-start(bf16[16,32,128]{2,1,0:T(8,128)(2,1)} %get-tuple-element.54) | copy-start | bytes 393220
  102.2 26.6 %copy-start.11 = (bf16[16,32,128]{2,1,0:T(8,128)(2,1)S(1)}, bf16[16,32,128]{2,1,0:T(8,128)(2,1)}, u32[]{:S(2)}) copy-start(bf16[16,32,128]{2,1,0:T(8,128)(2,1)} %get-tuple-element.55) | copy-start | bytes 393220
  102.2 28.4 %copy-start.10 = (bf16[16,32,128]{2,1,0:T(8,128)(2,1)S(1)}, bf16[16,32,128]{2,1,0:T(8,128)(2,1)}, u32[]{:S(2)}) copy-start(bf16[16,32,128]{2,1,0:T(8,128)(2,1)} %get-tuple-element.56) | copy-start | bytes 393220
  102.8 35.4 %copy-start = (bf16[64,16,256]{2,1,0:T(8,128)(2,1)S(1)}, bf16[64,16,256]{2,1,0:T(8,128)(2,1)}, u32[]{:S(2)}) copy-start(bf16[64,16,256]{2,1,0:T(8,128)(2,1)} %param.8) | copy-start | bytes 1572868
  102.8 35.4 %copy-start.2 = (f32[256]{0:T(256)S(1)}, f32[256]{0:T(256)}, u32[]{:S(2)}) copy-start(f32[256]{0:T(256)} %param.9) | copy-start | bytes 3076
  102.8 35.4 %copy-start.5 = (bf16[16,32,128]{2,1,0:T(8,128)(2,1)S(1)}, bf16[16,32,128]{2,1,0:T(8,128)(2,1)}, u32[]{:S(2)}) copy-start(bf16[16,32,128]{2,1,0:T(8,128)(2,1)} %get-tuple-element.53.p0_ref) | copy-start | bytes 393220
  119.1 2.9 %collective-permute-start.13 = (f32[80,128]{1,0:T(8,128)S(1)}, f32[80,128]{1,0:T(8,128)S(1)}, u32[]{:S(2)}, u32[]{:S(2)}) collective-permute-start(f32[80,128]{1,0:T(8,128)S(1)} %convert_reduce_fusion), channel_id=1, source_target_pairs={{0,2},{2,0},{4,6},{6,4},{1,3},{3,1},{5,7},{7,5},{8,10},{10,8},{12,... | collective-permute-start | bytes 122888 | tf_op jit(solution)/shard_map/ppermute | solution.py:614
  122.1 4.1 %collective-permute-start.14 = (f32[80,128]{1,0:T(8,128)S(1)}, f32[80,128]{1,0:T(8,128)S(1)}, u32[]{:S(2)}, u32[]{:S(2)}) collective-permute-start(f32[80,128]{1,0:T(8,128)S(1)} %add.22), channel_id=1, source_target_pairs={{0,6},{2,4},{4,2},{6,0},{1,7},{3,5},{5,3},{7,1},{8,14},{10,12},{12... | collective-permute-start | bytes 122888 | tf_op jit(solution)/shard_map/ppermute | solution.py:614
  126.2 5.5 %collective-permute-start.15 = (f32[80,128]{1,0:T(8,128)S(1)}, f32[80,128]{1,0:T(8,128)S(1)}, u32[]{:S(2)}, u32[]{:S(2)}) collective-permute-start(f32[80,128]{1,0:T(8,128)S(1)} %add.23.a_ref), channel_id=1, source_target_pairs={{0,1},{1,0},{2,3},{3,2},{4,5},{5,4},{6,7},{7,6},{8,9},{9,8},{10,11... | collective-permute-start | bytes 122888 | tf_op jit(solution)/shard_map/ppermute | solution.py:493
  128.9 9.0 %collective-permute-start.10 = (bf16[16,32,128]{2,1,0:T(8,128)(2,1)S(1)}, bf16[16,32,128]{2,1,0:T(8,128)(2,1)S(1)}, u32[]{:S(2)}, u32[]{:S(2)}) collective-permute-start(bf16[16,32,128]{2,1,0:T(8,128)(2,1)S(1)} %copy-done.12), channel_id=1, source_target_pairs={{0,32},{32,64},{64,96},{96,0},{1,33},{33,65},{65,97},{97,1},{2,34}... | collective-permute-start | bytes 393224 | tf_op jit(solution)/shard_map/ppermute | solution.py:510
  128.9 9.0 %collective-permute-start.11 = (bf16[16,32,128]{2,1,0:T(8,128)(2,1)S(1)}, bf16[16,32,128]{2,1,0:T(8,128)(2,1)S(1)}, u32[]{:S(2)}, u32[]{:S(2)}) collective-permute-start(bf16[16,32,128]{2,1,0:T(8,128)(2,1)S(1)} %copy-done.11), channel_id=1, source_target_pairs={{0,64},{32,96},{64,0},{96,32},{1,65},{33,97},{65,1},{97,33},{2,66}... | collective-permute-start | bytes 393224 | tf_op jit(solution)/shard_map/ppermute | solution.py:510
  130.6 7.6 %collective-permute-start.12 = (bf16[16,32,128]{2,1,0:T(8,128)(2,1)S(1)}, bf16[16,32,128]{2,1,0:T(8,128)(2,1)S(1)}, u32[]{:S(2)}, u32[]{:S(2)}) collective-permute-start(bf16[16,32,128]{2,1,0:T(8,128)(2,1)S(1)} %copy-done.10), channel_id=1, source_target_pairs={{0,96},{32,0},{64,32},{96,64},{1,97},{33,1},{65,33},{97,65},{2,98}... | collective-permute-start | bytes 393224 | tf_op jit(solution)/shard_map/ppermute | solution.py:510
  132.4 12.2 %all-to-all-start.4 = ((bf16[16,80,128]{2,1,0:T(8,128)(2,1)}), bf16[16,80,128]{2,1,0:T(8,128)(2,1)S(1)}, u32[]{:S(2)}, u32[]{:S(2)}) async-start(bf16[16,80,128]{2,1,0:T(8,128)(2,1)} %give.1), calls=%async_computation.4 | async-start | bytes 655360 | tf_op jit(solution)/shard_map/all_to_all | solution.py:489
  (6 other events, 9.2 us)

commit v2 on v1

--- a/solution.py
+++ b/solution.py
@@ -94,43 +94,45 @@
     )(x, gain, shift, wt, bias)
 
 
-def grad_kernel(s_ref, w_ref, gp_ref, st_ref, gb_ref, tall, held, sems):
-    ones = lax.broadcasted_iota(jnp.int32, (128, 128), 0) == lax.broadcasted_iota(
-        jnp.int32, (128, 128), 1
-    )
+def grad_kernel(s_ref, w_ref, gp_ref, st_ref, gb_ref, tall, held, st, sems):
     columns = []
     for d in range(4):
         count = jnp.zeros((32, 128), F32)
         for j in range(16):
             t = s_ref[d, j].astype(F32)
             count = count + t
-            st_ref[d * 32 : (d + 1) * 32, j * 128 : (j + 1) * 128] = (t * (1.0 / 256)).astype(
-                BF16
-            )
+            st[d * 32 : (d + 1) * 32, j * 128 : (j + 1) * 128] = (t * (1.0 / 256)).astype(BF16)
         columns.append(jnp.sum(count, axis=1, keepdims=True))
-    column = jnp.concatenate(columns, axis=0)
-    gb_ref[...] = jnp.sum(jnp.where(ones, column, 0.0), axis=0, keepdims=True)
-
-    for j in range(0, 16, 2):
-        g = dot(w_ref[...], st_ref[:, j * 128 : (j + 2) * 128], NN)
-        for jj in range(2):
-            tall[:, (j + jj) * 8 : (j + jj + 1) * 8, :] = g[
-                :, jj * 128 : (jj + 1) * 128
-            ].reshape(128, 8, 128)
+    copies = [pltpu.make_async_copy(st, st_ref, sems.at[8])]
+    copies[0].start()
 
     def relay(c, _):
         for e in range(32):
             held[c, e * 16 : (e + 1) * 16, :] = tall[
-                c * 4 + e // 8, pl.ds(e % 8, 16, stride=8), :
+                c * 4 + e // 8, pl.ds(e % 8 * 3, 16, stride=11), :
             ].astype(BF16)
         return 0
 
-    copies = []
-    for q in range(4):
-        lax.fori_loop(q * 8, (q + 1) * 8, relay, 0)
-        part = pl.ds(q * 8, 8)
-        copies.append(pltpu.make_async_copy(held.at[part], gp_ref.at[part], sems.at[q]))
-        copies[-1].start()
+    for half in range(2):
+        for j in range(0, 16, 2):
+            g = dot(
+                w_ref[half * 512 : (half + 1) * 512, :], st[:, j * 128 : (j + 2) * 128], NN
+            )
+            for jj in range(2):
+                for q in range(64):
+                    tall[half * 64 + q, pl.ds((j + jj) * 11, 8, stride=3), :] = g[
+                        q * 8 : (q + 1) * 8, jj * 128 : (jj + 1) * 128
+                    ]
+        for q in range(half * 4, half * 4 + 4):
+            lax.fori_loop(q * 4, (q + 1) * 4, relay, 0)
+            part = pl.ds(q * 4, 4)
+            copies.append(pltpu.make_async_copy(held.at[part], gp_ref.at[part], sems.at[q]))
+            copies[-1].start()
+    on = lax.broadcasted_iota(jnp.int32, (128, 128), 0) == lax.broadcasted_iota(
+        jnp.int32, (128, 128), 1
+    )
+    column = jnp.concatenate(columns, axis=0)
+    gb_ref[...] = jnp.sum(jnp.where(on, column, 0.0), axis=0, keepdims=True)
     for copy in copies:
         copy.wait()
 
@@ -144,12 +146,14 @@
             jax.ShapeDtypeStruct((1, 128), F32),
         ),
         in_specs=vmem(2),
-        out_specs=(*hbm(1), *vmem(2)),
+        out_specs=(*hbm(2), *vmem(1)),
         scratch_shapes=[
-            pltpu.VMEM((128, 128, 128), F32),
+            pltpu.VMEM((128, 192, 128), F32),
             pltpu.VMEM((32, 512, 128), BF16),
-            pltpu.SemaphoreType.DMA((4,)),
+            pltpu.VMEM((128, 2048), BF16),
+            pltpu.SemaphoreType.DMA((9,)),
         ],
+        compiler_params=limit(59),
         cost_estimate=cost(5),
         name="grad",
     )(s, w)
@@ -218,6 +222,7 @@
             pltpu.VMEM((16, 16, 16, 128), BF16),
             pltpu.SemaphoreType.DMA((8,)),
         ],
+        compiler_params=limit(59),
         cost_estimate=cost(5),
         name="left",
     )(*rs, gp)
@@ -289,6 +294,7 @@
             pltpu.VMEM((16, 16, 16, 128), BF16),
             pltpu.VMEM((4096, 256), BF16),
         ],
+        compiler_params=limit(59),
         cost_estimate=cost(5),
         name="right",
     )(near, far, gp)
@@ -297,14 +303,20 @@
 def outer_kernel(
     lt_ref, rt_ref, st_ref, w_ref, bias_ref,
     p0_ref, p1_ref, p2_ref, p3_ref, gw_ref,
-    tall, xs, lt, sems, pair,
+    tall, xs, lt, sems, pair, st, w, gw,
 ):
     depth = lax.axis_index("depth")
+    late = [
+        pltpu.make_async_copy(w_ref, w, sems.at[4]),
+        pltpu.make_async_copy(st_ref, st, sems.at[5]),
+    ]
     copies = []
     for q in range(4):
         part = pl.ds(q * 1024, 1024)
         copies.append(pltpu.make_async_copy(lt_ref.at[part], lt.at[part], sems.at[q]))
         copies[-1].start()
+    for copy in late:
+        copy.start()
     bias = column_of(bias_ref[...])
 
     def outer(k, _):
@@ -312,7 +324,7 @@
         o = dot(rt_ref[...], both, NT)
         for ch in range(2):
             for e in range(32):
-                tall[k * 8 + ch * 4 + e // 8, pl.ds(e % 8, 16, stride=8), :] = o[
+                tall[k * 8 + ch * 4 + e // 8, pl.ds(e % 8 * 3, 16, stride=11), :] = o[
                     e * 16 : (e + 1) * 16, ch * 128 : (ch + 1) * 128
                 ]
         return 0
@@ -323,30 +335,41 @@
 
     def convert(k, _):
         for j in range(16):
+            rows = [tall[k * 8 + q, pl.ds(j * 11, 8, stride=3), :] for q in range(8)]
             xs[pl.ds(pl.multiple_of(k * 64, 64), 64), j * 128 : (j + 1) * 128] = (
-                tall[pl.ds(k * 8, 8), j * 8 : (j + 1) * 8, :].reshape(64, 128).astype(BF16)
+                jnp.concatenate(rows, axis=0).astype(BF16)
             )
         return 0
 
     lax.fori_loop(0, 16, convert, 0)
+    for copy in late:
+        copy.wait()
 
     for j in range(0, 16, 2):
-        part = dot(w_ref[...], xs[:, j * 128 : (j + 2) * 128], TN)
+        part = dot(w[...], xs[:, j * 128 : (j + 2) * 128], TN)
         part = (part * (1.0 / 256) + bias).astype(BF16)
         for jj in range(2):
             for d in range(4):
                 pair[lax.rem(d - depth + 4, 4), j + jj] = part[
                     d * 32 : (d + 1) * 32, jj * 128 : (jj + 1) * 128
                 ]
+    outs = []
     for m, ref in enumerate((p0_ref, p1_ref, p2_ref, p3_ref)):
-        ref[...] = pair[m]
+        outs.append(pltpu.make_async_copy(pair.at[m], ref, sems.at[6 + m]))
+        outs[-1].start()
 
     def weight(k, _):
         at = pl.multiple_of(k * 256, 256)
-        gw_ref[pl.ds(at, 256), :] = dot(xs[pl.ds(at, 256), :], st_ref[...], NT).astype(BF16)
-        return 0
-
-    lax.fori_loop(0, 4, weight, 0)
+        gw[pl.ds(at, 256), :] = dot(xs[pl.ds(at, 256), :], st[...], NT).astype(BF16)
+        return 0
+
+    for half in range(2):
+        lax.fori_loop(half * 2, half * 2 + 2, weight, 0)
+        part = pl.ds(half * 512, 512)
+        outs.append(pltpu.make_async_copy(gw.at[part], gw_ref.at[part], sems.at[10 + half]))
+        outs[-1].start()
+    for copy in outs:
+        copy.wait()
 
 
 def outer_call(lt, rt, st, w, bias):
@@ -356,14 +379,17 @@
             *[jax.ShapeDtypeStruct((16, 32, 128), BF16)] * 4,
             jax.ShapeDtypeStruct((1024, 128), BF16),
         ),
-        in_specs=(*hbm(1), *vmem(4)),
-        out_specs=tuple(vmem(5)),
+        in_specs=(*hbm(1), *vmem(1), *hbm(2), *vmem(1)),
+        out_specs=hbm(5),
         scratch_shapes=[
-            pltpu.VMEM((128, 128, 128), F32),
+            pltpu.VMEM((128, 192, 128), F32),
             pltpu.VMEM((1024, 2048), BF16),
             pltpu.VMEM((4096, 256), BF16),
-            pltpu.SemaphoreType.DMA((4,)),
+            pltpu.SemaphoreType.DMA((12,)),
             pltpu.VMEM((4, 16, 32, 128), BF16),
+            pltpu.VMEM((128, 2048), BF16),
+            pltpu.VMEM((1024, 128), BF16),
+            pltpu.VMEM((1024, 128), BF16),
         ],
         cost_estimate=cost(11),
         name="outer",

time: 147 us -> 145 us (0.986)
  Pallas kernels: 43.2 us -> 41.6 us
  transfers between devices with their start and end apart: 20 -> 20, of which waited for: 10 -> 10; matrix products, arithmetic and copies ran while one was open for 2% -> 2% of each run, Pallas kernels for 29% -> 28%
where the time goes in v2:
time: 145 us; the launch traced here: 144 us
  starting transfers between devices  48 us (33%)
  Pallas kernels  41.6 us (29%)
  waiting for transfers between devices  30.9 us (21%)
  blocking collectives  16.2 us (11%)
  other arithmetic  3.49 us (2%)
  local copies, waits for them, and re-layouts  2.58 us (2%)
    all_to_all x4, starting transfers between devices, exchange(): return lax.all_to_all(value, axis, 0, 0, tiled=True)  22.4 us
    all_to_all x1, blocking collectives, exchange(): return lax.all_to_all(value, axis, 0, 0, tiled=True)  16.2 us
    ppermute x1, waiting for transfers between devices, step(): rights = [lax.ppermute(right, EVERY, pairs)]  12.3 us
    pallas_call x1, Pallas kernels, outer_call(): pl.pallas_call(outer_kernel, out_shape=(*[jax.ShapeDtypeStruct((16, 32, 1...  10.4 us
    pallas_call x1, Pallas kernels, left_call(): pl.pallas_call(left_kernel, out_shape=(jax.ShapeDtypeStruct((16, 16, 16,...  9.58 us
    ppermute x9, starting transfers between devices, rotate(): return lax.ppermute(value, axis, [(k, (k + by) % 4) for k in range(4)])  9.16 us
    ppermute x1, starting transfers between devices, step(): right_grad = lax.ppermute(right_grad, EVERY, [(b, a) for a, b in pairs])  6.73 us
    ppermute x2, waiting for transfers between devices, step(): total = total + lax.ppermute(total, 'col_0', [(k, k ^ m) for k in range(4)])  6.27 us
  transfers between devices with their start and end apart: 20, of which 10 were waited for; matrix products, arithmetic and copies ran while one was open for 2% of the time, Pallas kernels for 28%

profile of v2, /device:TPU:1, one launch (start us, length us, event | category | flops | bytes accessed | tf_op | source)
XLA Modules:
  0.0 143.8 jit_solution(13554728678902907721)
XLA Ops:
  0.6 5.0 %all-to-all-start = ((bf16[4,16,32,128]{3,2,1,0:T(8,128)(2,1)}), bf16[4,16,32,128]{3,2,1,0:T(8,128)(2,1)S(1)}, u32[]{:S(2)}, u32[]{:S(2)}) async-start(bf16[4,16,32,128]{3,2,1,0:T(8,128)(2,1)} %bitcast.23), calls=%async_computation | async-start | bytes 1048576 | tf_op jit(solution)/shard_map/all_to_all | solution.py:515
  5.6 4.5 %sides.1 = (bf16[16,16,16,128]{3,2,1,0:T(8,128)(2,1)}, bf16[16,16,128]{2,1,0:T(8,128)(2,1)}, bf16[1024,512]{1,0:T(8,128)(2,1)}) custom-call(bf16[1024,256]{1,0:T(8,128)(2,1)} %bitcast.16, f32[1,256]{1,0:T(1,128)} %bitcast.21, f32[1,256]{1,0:T(1,128)} %bitcast.24, bf16[64,256]{1,0:T(8,128)(2,1)} %bitcast.18, f32[1,64]{1,0:T(1,128)} %bitcast.25), custom_call_target="tpu_custom_call" | custom-call | flops 1600000000 | bytes 1000000 | tf_op jit(solution)/shard_map/sides/pallas_call | solution.py:82
  10.1 3.8 %all-to-all-done.s_ref = bf16[4,16,32,128]{3,2,1,0:T(8,128)(2,1)S(1)} async-done(((bf16[4,16,32,128]{3,2,1,0:T(8,128)(2,1)}), bf16[4,16,32,128]{3,2,1,0:T(8,128)(2,1)S(1)}, u32[]{:S(2)}, u32[]{:S(2)}) %all-to-all-start) | async-done | bytes 524320 | tf_op jit(solution)/shard_map/all_to_all | solution.py:515
  14.0 5.7 %all-to-all-start.2 = ((bf16[16,16,16,128]{3,2,1,0:T(8,128)(2,1)}), bf16[16,16,16,128]{3,2,1,0:T(8,128)(2,1)S(1)}, u32[]{:S(2)}, u32[]{:S(2)}) async-start(bf16[16,16,16,128]{3,2,1,0:T(8,128)(2,1)} %get-tuple-element.41), calls=%async_computation.2 | async-start | bytes 2097152 | tf_op jit(solution)/shard_map/all_to_all | solution.py:515
  19.7 5.8 %collective-permute-start = (bf16[16,16,128]{2,1,0:T(8,128)(2,1)S(1)}, bf16[16,16,128]{2,1,0:T(8,128)(2,1)S(1)}, u32[]{:S(2)}, u32[]{:S(2)}) collective-permute-start(bf16[16,16,128]{2,1,0:T(8,128)(2,1)S(1)} %copy-done.17), channel_id=1, source_target_pairs={{0,0},{1,32},{2,64},{3,96},{4,1},{5,33},{6,65},{7,97},{8,2},{9,34}... | collective-permute-start | bytes 196616 | tf_op jit(solution)/shard_map/ppermute | solution.py:617
  25.6 12.3 %collective-permute-done.r0_ref = bf16[16,16,128]{2,1,0:T(8,128)(2,1)S(1)} collective-permute-done((bf16[16,16,128]{2,1,0:T(8,128)(2,1)S(1)}, bf16[16,16,128]{2,1,0:T(8,128)(2,1)S(1)}, u32[]{:S(2)}, u32[]{:S(2)}) %collective-permute-start) | collective-permute-done | bytes 65568 | tf_op jit(solution)/shard_map/ppermute | solution.py:617
  37.9 2.7 %collective-permute-start.3 = (bf16[16,16,128]{2,1,0:T(8,128)(2,1)S(1)}, bf16[16,16,128]{2,1,0:T(8,128)(2,1)S(1)}, u32[]{:S(2)}, u32[]{:S(2)}) collective-permute-start(bf16[16,16,128]{2,1,0:T(8,128)(2,1)S(1)} %collective-permute-done.r0_ref), channel_id=1, source_target_pairs={{0,24},{8,0},{16,8},{24,16},{1,25},{9,1},{17,9},{25,17},{2,26},{10... | collective-permute-start | bytes 196616 | tf_op jit(solution)/shard_map/ppermute | solution.py:536
  40.6 4.9 %grad.1 = (bf16[32,512,128]{2,1,0:T(8,128)(2,1)}, bf16[128,2048]{1,0:T(8,128)(2,1)}, f32[1,128]{1,0:T(1,128)}) custom-call(bf16[4,16,32,128]{3,2,1,0:T(8,128)(2,1)} %copy-done.8, bf16[1024,128]{1,0:T(8,128)(2,1)} %w_ref.3), custom_call_target="tpu_custom_call" | custom-call | flops 2000000000 | bytes 1000000 | tf_op jit(solution)/shard_map/grad/pallas_call | solution.py:141
  46.1 9.6 %left.1 = (bf16[16,16,16,128]{3,2,1,0:T(8,128)(2,1)}, bf16[16,16,16,128]{3,2,1,0:T(8,128)(2,1)}, bf16[512,256]{1,0:T(8,128)(2,1)}) custom-call(bf16[16,16,128]{2,1,0:T(8,128)(2,1)} %copy-done.13, bf16[16,16,128]{2,1,0:T(8,128)(2,1)} %copy-done.14, bf16[16,16,128]{2,1,0:T(8,128)(2,1)} %copy-done.15, bf16[16,16,128]{2,1,0:T(8,128)(2,1)} %copy-done.16, ...), custom_call_target="tpu_custom_call" | custom-call | flops 2000000000 | bytes 1000000 | tf_op jit(solution)/shard_map/left/pallas_call | solution.py:208
  56.3 2.4 %collective-permute-done.4 = bf16[16,16,16,128]{3,2,1,0:T(8,128)(2,1)S(1)} collective-permute-done((bf16[16,16,16,128]{3,2,1,0:T(8,128)(2,1)}, bf16[16,16,16,128]{3,2,1,0:T(8,128)(2,1)S(1)}, u32[]{:S(2)}, u32[]{:S(2)}) %collective-permute-start.4) | collective-permute-done | bytes 1048608 | tf_op jit(solution)/shard_map/ppermute | solution.py:519
  58.7 2.5 %add_convert_fusion = bf16[16,16,16,128]{3,2,1,0:T(8,128)(2,1)} fusion(bf16[16,16,16,128]{3,2,1,0:T(8,128)(2,1)S(1)} %collective-permute-done.4, bf16[16,16,16,128]{3,2,1,0:T(8,128)(2,1)} %get-tuple-element.39), kind=kLoop, calls=%fused_computation | loop fusion | flops 2097152 | bytes 3145728 | tf_op jit(solution)/shard_map/convert_element_type | solution.py:625
  61.2 7.7 %all-to-all-start.1 = ((bf16[16,16,16,128]{3,2,1,0:T(8,128)(2,1)}), bf16[16,16,16,128]{3,2,1,0:T(8,128)(2,1)S(1)}, u32[]{:S(2)}, u32[]{:S(2)}) async-start(bf16[16,16,16,128]{3,2,1,0:T(8,128)(2,1)} %add_convert_fusion), calls=%async_computation.1 | async-start | bytes 2097152 | tf_op jit(solution)/shard_map/all_to_all | solution.py:515
  68.9 1.0 copy-done.9
  69.9 5.3 %right.1 = (bf16[16,16,128]{2,1,0:T(8,128)(2,1)}, bf16[16,16,128]{2,1,0:T(8,128)(2,1)}, bf16[16,16,128]{2,1,0:T(8,128)(2,1)}, bf16[16,16,128]{2,1,0:T(8,128)(2,1)}, bf16[4096,256]{1,0:T(8,128)(2,1)}) custom-call(bf16[16,16,16,128]{3,2,1,0:T(8,128)(2,1)} %copy-done.7, bf16[16,16,16,128]{3,2,1,0:T(8,128)(2,1)} %copy-done.9, ...), custom_call_target="tpu_custom_call" | custom-call | flops 2000000000 | bytes 1000000 | tf_op jit(solution)/shard_map/right/pallas_call | solution.py:281
  75.2 1.3 collective-permute-start.6
  76.7 2.2 %collective-permute-start.8 = (bf16[16,16,128]{2,1,0:T(8,128)(2,1)}, bf16[16,16,128]{2,1,0:T(8,128)(2,1)S(1)}, u32[]{:S(2)}, u32[]{:S(2)}) collective-permute-start(bf16[16,16,128]{2,1,0:T(8,128)(2,1)} %get-tuple-element.45), channel_id=1, source_target_pairs={{0,24},{8,0},{16,8},{24,16},{1,25},{9,1},{17,9},{25,17},{2,26},{10... | collective-permute-start | bytes 196616 | tf_op jit(solution)/shard_map/ppermute | solution.py:536
  78.9 1.2 collective-permute-done.6
  80.1 1.5 %collective-permute-done.7 = bf16[16,16,128]{2,1,0:T(8,128)(2,1)S(1)} collective-permute-done((bf16[16,16,128]{2,1,0:T(8,128)(2,1)}, bf16[16,16,128]{2,1,0:T(8,128)(2,1)S(1)}, u32[]{:S(2)}, u32[]{:S(2)}) %collective-permute-start.7) | collective-permute-done | bytes 65568 | tf_op jit(solution)/shard_map/ppermute | solution.py:536
  81.6 0.9 add_convert_fusion.1
  82.5 6.7 %collective-permute-start.9 = (bf16[16,16,128]{2,1,0:T(8,128)(2,1)S(1)}, bf16[16,16,128]{2,1,0:T(8,128)(2,1)S(1)}, u32[]{:S(2)}, u32[]{:S(2)}) collective-permute-start(bf16[16,16,128]{2,1,0:T(8,128)(2,1)S(1)} %add_convert_fusion.1), channel_id=1, source_target_pairs={{0,0},{32,1},{64,2},{96,3},{1,4},{33,5},{65,6},{97,7},{2,8},{34,9}... | collective-permute-start | bytes 196616 | tf_op jit(solution)/shard_map/ppermute | solution.py:632
  89.2 10.4 %outer.1 = (bf16[16,32,128]{2,1,0:T(8,128)(2,1)}, bf16[16,32,128]{2,1,0:T(8,128)(2,1)}, bf16[16,32,128]{2,1,0:T(8,128)(2,1)}, bf16[16,32,128]{2,1,0:T(8,128)(2,1)}, bf16[1024,128]{1,0:T(8,128)(2,1)}) custom-call(bf16[4096,256]{1,0:T(8,128)(2,1)} %get-tuple-element.48.lt_ref, bf16[512,256]{1,0:T(8,128)(2,1)} %get-tuple-element.49.rt_ref, ...), custom_call_target="tpu_custom_call" | custom-call | flops 4400000000 | bytes 1000000 | tf_op jit(solution)/shard_map/outer/pallas_call | solution.py:376
  99.7 0.9 copy-done.4
  101.3 16.2 %all_to_all.25 = bf16[16,80,128]{2,1,0:T(8,128)(2,1)S(1)} all-to-all(bf16[16,80,128]{2,1,0:T(8,128)(2,1)S(1)} %get-tuple-element.59), channel_id=1, replica_groups=mesh['depth'=4,'row'=4,'col_0'=4,'col_1'=2] {'depth','row'}, dimensions={0} | all-to-all | bytes 655360 | tf_op jit(solution)/shard_map/all_to_all | solution.py:515
  118.2 2.2 %collective-permute-done.13 = f32[80,128]{1,0:T(8,128)S(1)} collective-permute-done((f32[80,128]{1,0:T(8,128)S(1)}, f32[80,128]{1,0:T(8,128)S(1)}, u32[]{:S(2)}, u32[]{:S(2)}) %collective-permute-start.13) | collective-permute-done | bytes 40992 | tf_op jit(solution)/shard_map/ppermute | solution.py:640
  120.5 4.1 %collective-permute-done.14 = f32[80,128]{1,0:T(8,128)S(1)} collective-permute-done((f32[80,128]{1,0:T(8,128)S(1)}, f32[80,128]{1,0:T(8,128)S(1)}, u32[]{:S(2)}, u32[]{:S(2)}) %collective-permute-start.14) | collective-permute-done | bytes 40992 | tf_op jit(solution)/shard_map/ppermute | solution.py:640
  124.5 2.7 %collective-permute-start.15 = (f32[80,128]{1,0:T(8,128)S(1)}, f32[80,128]{1,0:T(8,128)S(1)}, u32[]{:S(2)}, u32[]{:S(2)}) collective-permute-start(f32[80,128]{1,0:T(8,128)S(1)} %add.23.a_ref), channel_id=1, source_target_pairs={{0,1},{1,0},{2,3},{3,2},{4,5},{5,4},{6,7},{7,6},{8,9},{9,8},{10,11... | collective-permute-start | bytes 122888 | tf_op jit(solution)/shard_map/ppermute | solution.py:519
  127.3 1.8 %collective-permute-start.11 = (bf16[16,32,128]{2,1,0:T(8,128)(2,1)S(1)}, bf16[16,32,128]{2,1,0:T(8,128)(2,1)S(1)}, u32[]{:S(2)}, u32[]{:S(2)}) collective-permute-start(bf16[16,32,128]{2,1,0:T(8,128)(2,1)S(1)} %copy-done.11), channel_id=1, source_target_pairs={{0,64},{32,96},{64,0},{96,32},{1,65},{33,97},{65,1},{97,33},{2,66}... | collective-permute-start | bytes 393224 | tf_op jit(solution)/shard_map/ppermute | solution.py:536
  129.0 1.0 collective-permute-start.12
  130.8 3.9 %all-to-all-start.4 = ((bf16[16,80,128]{2,1,0:T(8,128)(2,1)}), bf16[16,80,128]{2,1,0:T(8,128)(2,1)S(1)}, u32[]{:S(2)}, u32[]{:S(2)}) async-start(bf16[16,80,128]{2,1,0:T(8,128)(2,1)} %give.1), calls=%async_computation.4 | async-start | bytes 655360 | tf_op jit(solution)/shard_map/all_to_all | solution.py:515
  134.7 1.6 %collective-permute-done.10.p1_ref = bf16[16,32,128]{2,1,0:T(8,128)(2,1)S(1)} collective-permute-done((bf16[16,32,128]{2,1,0:T(8,128)(2,1)S(1)}, bf16[16,32,128]{2,1,0:T(8,128)(2,1)S(1)}, u32[]{:S(2)}, u32[]{:S(2)}) %collective-permute-start.10) | collective-permute-done | bytes 131104 | tf_op jit(solution)/shard_map/ppermute | solution.py:536
  136.6 4.8 %norm.1 = (bf16[1024,256]{1,0:T(8,128)(2,1)}, bf16[64,32,128]{2,1,0:T(8,128)(2,1)}) custom-call(bf16[1024,256]{1,0:T(8,128)(2,1)S(1)} %bitcast.17, f32[1,256]{1,0:T(1,128)S(1)} %bitcast.22, bf16[64,256]{1,0:T(8,128)(2,1)S(1)} %bitcast.20, bf16[64,1024]{1,0:T(8,128)(2,1)S(1)} %get-tuple-element.52.grad_ref, bf16[16,32,128]{2,1,0:T(8,128)(2,1)S(1)} %copy-done.5, ...), custom_call_target="tpu_custom_call" | custom-call | flops 2000000000 | bytes 1000000 | tf_op jit(solution)/shard_map/norm/pallas_call | solution.py:499
  141.4 1.5 %all-to-all-done.4.all_ref = bf16[16,80,128]{2,1,0:T(8,128)(2,1)S(1)} async-done(((bf16[16,80,128]{2,1,0:T(8,128)(2,1)}), bf16[16,80,128]{2,1,0:T(8,128)(2,1)S(1)}, u32[]{:S(2)}, u32[]{:S(2)}) %all-to-all-start.4) | async-done | bytes 327712 | tf_op jit(solution)/shard_map/all_to_all | solution.py:515
  (59 shorter events, 4.8 us)
Async XLA Ops:
  0.6 13.3 %all-to-all-start = ((bf16[4,16,32,128]{3,2,1,0:T(8,128)(2,1)}), bf16[4,16,32,128]{3,2,1,0:T(8,128)(2,1)S(1)}, u32[]{:S(2)}, u32[]{:S(2)}) async-start(bf16[4,16,32,128]{3,2,1,0:T(8,128)(2,1)} %bitcast.23), calls=%async_computation | async-start | bytes 1048576 | tf_op jit(solution)/shard_map/all_to_all | solution.py:515
  10.1 9.6 %copy-start.17 = (bf16[16,16,128]{2,1,0:T(8,128)(2,1)S(1)}, bf16[16,16,128]{2,1,0:T(8,128)(2,1)}, u32[]{:S(2)}) copy-start(bf16[16,16,128]{2,1,0:T(8,128)(2,1)} %get-tuple-element.37) | copy-start | bytes 196612
  14.0 26.6 %copy-start.8 = (bf16[4,16,32,128]{3,2,1,0:T(8,128)(2,1)}, bf16[4,16,32,128]{3,2,1,0:T(8,128)(2,1)S(1)}, u32[]{:S(2)}) copy-start(bf16[4,16,32,128]{3,2,1,0:T(8,128)(2,1)S(1)} %all-to-all-done.s_ref) | copy-start | bytes 1572868
  14.0 41.8 %all-to-all-start.2 = ((bf16[16,16,16,128]{3,2,1,0:T(8,128)(2,1)}), bf16[16,16,16,128]{3,2,1,0:T(8,128)(2,1)S(1)}, u32[]{:S(2)}, u32[]{:S(2)}) async-start(bf16[16,16,16,128]{3,2,1,0:T(8,128)(2,1)} %get-tuple-element.41), calls=%async_computation.2 | async-start | bytes 2097152 | tf_op jit(solution)/shard_map/all_to_all | solution.py:515
  19.7 18.2 %collective-permute-start = (bf16[16,16,128]{2,1,0:T(8,128)(2,1)S(1)}, bf16[16,16,128]{2,1,0:T(8,128)(2,1)S(1)}, u32[]{:S(2)}, u32[]{:S(2)}) collective-permute-start(bf16[16,16,128]{2,1,0:T(8,128)(2,1)S(1)} %copy-done.17), channel_id=1, source_target_pairs={{0,0},{1,32},{2,64},{3,96},{4,1},{5,33},{6,65},{7,97},{8,2},{9,34}... | collective-permute-start | bytes 196616 | tf_op jit(solution)/shard_map/ppermute | solution.py:617
  37.9 7.6 %copy-start.13 = (bf16[16,16,128]{2,1,0:T(8,128)(2,1)}, bf16[16,16,128]{2,1,0:T(8,128)(2,1)S(1)}, u32[]{:S(2)}) copy-start(bf16[16,16,128]{2,1,0:T(8,128)(2,1)S(1)} %collective-permute-done.r0_ref) | copy-start | bytes 196612
  37.9 7.6 %collective-permute-start.1 = (bf16[16,16,128]{2,1,0:T(8,128)(2,1)S(1)}, bf16[16,16,128]{2,1,0:T(8,128)(2,1)S(1)}, u32[]{:S(2)}, u32[]{:S(2)}) collective-permute-start(bf16[16,16,128]{2,1,0:T(8,128)(2,1)S(1)} %collective-permute-done.r0_ref), channel_id=1, source_target_pairs={{0,8},{8,16},{16,24},{24,0},{1,9},{9,17},{17,25},{25,1},{2,10},{10... | collective-permute-start | bytes 196616 | tf_op jit(solution)/shard_map/ppermute | solution.py:536
  37.9 7.6 %collective-permute-start.2 = (bf16[16,16,128]{2,1,0:T(8,128)(2,1)S(1)}, bf16[16,16,128]{2,1,0:T(8,128)(2,1)S(1)}, u32[]{:S(2)}, u32[]{:S(2)}) collective-permute-start(bf16[16,16,128]{2,1,0:T(8,128)(2,1)S(1)} %collective-permute-done.r0_ref), channel_id=1, source_target_pairs={{0,16},{8,24},{16,0},{24,8},{1,17},{9,25},{17,1},{25,9},{2,18},{10... | collective-permute-start | bytes 196616 | tf_op jit(solution)/shard_map/ppermute | solution.py:536
  37.9 7.6 %collective-permute-start.3 = (bf16[16,16,128]{2,1,0:T(8,128)(2,1)S(1)}, bf16[16,16,128]{2,1,0:T(8,128)(2,1)S(1)}, u32[]{:S(2)}, u32[]{:S(2)}) collective-permute-start(bf16[16,16,128]{2,1,0:T(8,128)(2,1)S(1)} %collective-permute-done.r0_ref), channel_id=1, source_target_pairs={{0,24},{8,0},{16,8},{24,16},{1,25},{9,1},{17,9},{25,17},{2,26},{10... | collective-permute-start | bytes 196616 | tf_op jit(solution)/shard_map/ppermute | solution.py:536
  55.7 3.0 %collective-permute-start.4 = (bf16[16,16,16,128]{3,2,1,0:T(8,128)(2,1)}, bf16[16,16,16,128]{3,2,1,0:T(8,128)(2,1)S(1)}, u32[]{:S(2)}, u32[]{:S(2)}) collective-permute-start(bf16[16,16,16,128]{3,2,1,0:T(8,128)(2,1)} %get-tuple-element.40), channel_id=1, source_target_pairs={{0,1},{1,0},{2,3},{3,2},{4,5},{5,4},{6,7},{7,6},{8,9},{9,8},{10,11... | collective-permute-start | bytes 3145736 | tf_op jit(solution)/shard_map/ppermute | solution.py:519
  55.8 13.1 %collective-permute-start.5 = (bf16[16,16,16,128]{3,2,1,0:T(8,128)(2,1)S(1)}, bf16[16,16,16,128]{3,2,1,0:T(8,128)(2,1)S(1)}, u32[]{:S(2)}, u32[]{:S(2)}) collective-permute-start(bf16[16,16,16,128]{3,2,1,0:T(8,128)(2,1)S(1)} %all-to-all-done.2.near_ref), channel_id=1, source_target_pairs={{0,1},{1,0},{2,3},{3,2},{4,5},{5,4},{6,7},{7,6},{8,9},{9,8},{10,11... | collective-permute-start | bytes 3145736 | tf_op jit(solution)/shard_map/ppermute | solution.py:519
  61.2 38.4 %all-to-all-start.1 = ((bf16[16,16,16,128]{3,2,1,0:T(8,128)(2,1)}), bf16[16,16,16,128]{3,2,1,0:T(8,128)(2,1)S(1)}, u32[]{:S(2)}, u32[]{:S(2)}) async-start(bf16[16,16,16,128]{3,2,1,0:T(8,128)(2,1)} %add_convert_fusion), calls=%async_computation.1 | async-start | bytes 2097152 | tf_op jit(solution)/shard_map/all_to_all | solution.py:515
  75.2 4.9 %collective-permute-start.6 = (bf16[16,16,128]{2,1,0:T(8,128)(2,1)}, bf16[16,16,128]{2,1,0:T(8,128)(2,1)S(1)}, u32[]{:S(2)}, u32[]{:S(2)}) collective-permute-start(bf16[16,16,128]{2,1,0:T(8,128)(2,1)} %get-tuple-element.43), channel_id=1, source_target_pairs={{0,8},{8,16},{16,24},{24,0},{1,9},{9,17},{17,25},{25,1},{2,10},{10... | collective-permute-start | bytes 196616 | tf_op jit(solution)/shard_map/ppermute | solution.py:536
  76.4 5.1 %collective-permute-start.7 = (bf16[16,16,128]{2,1,0:T(8,128)(2,1)}, bf16[16,16,128]{2,1,0:T(8,128)(2,1)S(1)}, u32[]{:S(2)}, u32[]{:S(2)}) collective-permute-start(bf16[16,16,128]{2,1,0:T(8,128)(2,1)} %get-tuple-element.44), channel_id=1, source_target_pairs={{0,16},{8,24},{16,0},{24,8},{1,17},{9,25},{17,1},{25,9},{2,18},{10... | collective-permute-start | bytes 196616 | tf_op jit(solution)/shard_map/ppermute | solution.py:536
  76.7 4.9 %collective-permute-start.8 = (bf16[16,16,128]{2,1,0:T(8,128)(2,1)}, bf16[16,16,128]{2,1,0:T(8,128)(2,1)S(1)}, u32[]{:S(2)}, u32[]{:S(2)}) collective-permute-start(bf16[16,16,128]{2,1,0:T(8,128)(2,1)} %get-tuple-element.45), channel_id=1, source_target_pairs={{0,24},{8,0},{16,8},{24,16},{1,25},{9,1},{17,9},{25,17},{2,26},{10... | collective-permute-start | bytes 196616 | tf_op jit(solution)/shard_map/ppermute | solution.py:536
  82.5 17.2 %collective-permute-start.9 = (bf16[16,16,128]{2,1,0:T(8,128)(2,1)S(1)}, bf16[16,16,128]{2,1,0:T(8,128)(2,1)S(1)}, u32[]{:S(2)}, u32[]{:S(2)}) collective-permute-start(bf16[16,16,128]{2,1,0:T(8,128)(2,1)S(1)} %add_convert_fusion.1), channel_id=1, source_target_pairs={{0,0},{32,1},{64,2},{96,3},{1,4},{33,5},{65,6},{97,7},{2,8},{34,9}... | collective-permute-start | bytes 196616 | tf_op jit(solution)/shard_map/ppermute | solution.py:632
  89.2 10.5 %copy-start.1 = (bf16[256,64]{0,1:T(8,128)(2,1)S(1)}, bf16[256,64]{0,1:T(8,128)(2,1)}, u32[]{:S(2)}) copy-start(bf16[256,64]{0,1:T(8,128)(2,1)} %param.11) | copy-start | bytes 98308
  89.2 10.5 %copy-start.3 = (bf16[1024,512]{1,0:T(8,128)(2,1)S(1)}, bf16[1024,512]{1,0:T(8,128)(2,1)}, u32[]{:S(2)}) copy-start(bf16[1024,512]{1,0:T(8,128)(2,1)} %get-tuple-element.46.normed_ref) | copy-start | bytes 3145732
  89.2 10.5 %copy-start.6 = (f32[1,128]{1,0:T(1,128)S(1)}, f32[1,128]{1,0:T(1,128)}, u32[]{:S(2)}) copy-start(f32[1,128]{1,0:T(1,128)} %get-tuple-element.47.count_ref) | copy-start | bytes 1540
  100.6 26.6 %copy-start.12 = (bf16[16,32,128]{2,1,0:T(8,128)(2,1)S(1)}, bf16[16,32,128]{2,1,0:T(8,128)(2,1)}, u32[]{:S(2)}) copy-start(bf16[16,32,128]{2,1,0:T(8,128)(2,1)} %get-tuple-element.54) | copy-start | bytes 393220
  100.6 26.6 %copy-start.11 = (bf16[16,32,128]{2,1,0:T(8,128)(2,1)S(1)}, bf16[16,32,128]{2,1,0:T(8,128)(2,1)}, u32[]{:S(2)}) copy-start(bf16[16,32,128]{2,1,0:T(8,128)(2,1)} %get-tuple-element.55) | copy-start | bytes 393220
  100.6 28.4 %copy-start.10 = (bf16[16,32,128]{2,1,0:T(8,128)(2,1)S(1)}, bf16[16,32,128]{2,1,0:T(8,128)(2,1)}, u32[]{:S(2)}) copy-start(bf16[16,32,128]{2,1,0:T(8,128)(2,1)} %get-tuple-element.56) | copy-start | bytes 393220
  101.2 35.4 %copy-start = (bf16[64,16,256]{2,1,0:T(8,128)(2,1)S(1)}, bf16[64,16,256]{2,1,0:T(8,128)(2,1)}, u32[]{:S(2)}) copy-start(bf16[64,16,256]{2,1,0:T(8,128)(2,1)} %param.8) | copy-start | bytes 1572868
  101.2 35.3 %copy-start.2 = (f32[256]{0:T(256)S(1)}, f32[256]{0:T(256)}, u32[]{:S(2)}) copy-start(f32[256]{0:T(256)} %param.9) | copy-start | bytes 3076
  101.3 35.3 %copy-start.5 = (bf16[16,32,128]{2,1,0:T(8,128)(2,1)S(1)}, bf16[16,32,128]{2,1,0:T(8,128)(2,1)}, u32[]{:S(2)}) copy-start(bf16[16,32,128]{2,1,0:T(8,128)(2,1)} %get-tuple-element.53.p0_ref) | copy-start | bytes 393220
  117.5 2.9 %collective-permute-start.13 = (f32[80,128]{1,0:T(8,128)S(1)}, f32[80,128]{1,0:T(8,128)S(1)}, u32[]{:S(2)}, u32[]{:S(2)}) collective-permute-start(f32[80,128]{1,0:T(8,128)S(1)} %convert_reduce_fusion), channel_id=1, source_target_pairs={{0,2},{2,0},{4,6},{6,4},{1,3},{3,1},{5,7},{7,5},{8,10},{10,8},{12,... | collective-permute-start | bytes 122888 | tf_op jit(solution)/shard_map/ppermute | solution.py:640
  120.5 4.1 %collective-permute-start.14 = (f32[80,128]{1,0:T(8,128)S(1)}, f32[80,128]{1,0:T(8,128)S(1)}, u32[]{:S(2)}, u32[]{:S(2)}) collective-permute-start(f32[80,128]{1,0:T(8,128)S(1)} %add.22), channel_id=1, source_target_pairs={{0,6},{2,4},{4,2},{6,0},{1,7},{3,5},{5,3},{7,1},{8,14},{10,12},{12... | collective-permute-start | bytes 122888 | tf_op jit(solution)/shard_map/ppermute | solution.py:640
  124.5 5.5 %collective-permute-start.15 = (f32[80,128]{1,0:T(8,128)S(1)}, f32[80,128]{1,0:T(8,128)S(1)}, u32[]{:S(2)}, u32[]{:S(2)}) collective-permute-start(f32[80,128]{1,0:T(8,128)S(1)} %add.23.a_ref), channel_id=1, source_target_pairs={{0,1},{1,0},{2,3},{3,2},{4,5},{5,4},{6,7},{7,6},{8,9},{9,8},{10,11... | collective-permute-start | bytes 122888 | tf_op jit(solution)/shard_map/ppermute | solution.py:519
  127.2 9.0 %collective-permute-start.10 = (bf16[16,32,128]{2,1,0:T(8,128)(2,1)S(1)}, bf16[16,32,128]{2,1,0:T(8,128)(2,1)S(1)}, u32[]{:S(2)}, u32[]{:S(2)}) collective-permute-start(bf16[16,32,128]{2,1,0:T(8,128)(2,1)S(1)} %copy-done.12), channel_id=1, source_target_pairs={{0,32},{32,64},{64,96},{96,0},{1,33},{33,65},{65,97},{97,1},{2,34}... | collective-permute-start | bytes 393224 | tf_op jit(solution)/shard_map/ppermute | solution.py:536
  127.3 9.0 %collective-permute-start.11 = (bf16[16,32,128]{2,1,0:T(8,128)(2,1)S(1)}, bf16[16,32,128]{2,1,0:T(8,128)(2,1)S(1)}, u32[]{:S(2)}, u32[]{:S(2)}) collective-permute-start(bf16[16,32,128]{2,1,0:T(8,128)(2,1)S(1)} %copy-done.11), channel_id=1, source_target_pairs={{0,64},{32,96},{64,0},{96,32},{1,65},{33,97},{65,1},{97,33},{2,66}... | collective-permute-start | bytes 393224 | tf_op jit(solution)/shard_map/ppermute | solution.py:536
  129.0 7.6 %collective-permute-start.12 = (bf16[16,32,128]{2,1,0:T(8,128)(2,1)S(1)}, bf16[16,32,128]{2,1,0:T(8,128)(2,1)S(1)}, u32[]{:S(2)}, u32[]{:S(2)}) collective-permute-start(bf16[16,32,128]{2,1,0:T(8,128)(2,1)S(1)} %copy-done.10), channel_id=1, source_target_pairs={{0,96},{32,0},{64,32},{96,64},{1,97},{33,1},{65,33},{97,65},{2,98}... | collective-permute-start | bytes 393224 | tf_op jit(solution)/shard_map/ppermute | solution.py:536
  130.8 12.2 %all-to-all-start.4 = ((bf16[16,80,128]{2,1,0:T(8,128)(2,1)}), bf16[16,80,128]{2,1,0:T(8,128)(2,1)S(1)}, u32[]{:S(2)}, u32[]{:S(2)}) async-start(bf16[16,80,128]{2,1,0:T(8,128)(2,1)} %give.1), calls=%async_computation.4 | async-start | bytes 655360 | tf_op jit(solution)/shard_map/all_to_all | solution.py:515
  (6 other events, 9.2 us)
